TPU v7x, 128 devices: a whole 4x4x4 slice. The times are simulated.
128 devices in a mesh: row: 16 (over z_hi, x, core), col: 8 (over y, z_lo).
Axes of the slice: x: 4, y: 4, z: 4 (z_hi: 2, z_lo: 2; z = z_hi * 2 + z_lo), core: 2. Of those that a mesh axis runs over, the one named last changes fastest.
Arguments:
- pair: bfloat16 [512, 512, 128], P('row', 'col'), may hold values from -6 to 6
- cotangent: bfloat16 [512, 512, 128], P('row', 'col'), may hold values from -6 to 6
- length: int32 [1], replicated, may hold values from 256 to 512
- norm_gain: float32 [128], replicated, may hold values from 0.1 to 1.9
- norm_bias: float32 [128], replicated, may hold values from -1.5 to 1.5
- left_weight: bfloat16 [128, 256], replicated, may hold values from -0.5 to 0.5
- right_weight: bfloat16 [128, 256], replicated, may hold values from -0.5 to 0.5
- gate_weight: bfloat16 [128, 128], replicated, may hold values from -0.5 to 0.5
- out_gain: float32 [128], replicated, may hold values from 0.1 to 1.9
- out_bias: float32 [128], replicated, may hold values from -2 to 2
- out_weight: bfloat16 [128, 128], replicated, may hold values from -0.5 to 0.5
Outputs:
- update: bfloat16 [512, 512, 128], P('row', 'col')
- grad_pair: bfloat16 [512, 512, 128], P('row', 'col')
- grad_left: float32 [128, 256], replicated
- grad_right: float32 [128, 256], replicated
- grad_gating: float32 [128, 128], replicated
- grad_output: float32 [128, 128], replicated
- grad_norms: float32 [4, 128], replicated
Inputs may be any that keep to these rules, and one draw needn't show every extreme that they name: Tokens at positions 511 down to length are padding.
All inputs are finite; a program needn't handle non-finite values.
Results may differ from a plain program's by a relative error of at most 0.014.
Values may be sent and summed in bfloat16 or wider, within the bound.
A program may use at most 128 MiB of HBM per device.

v0:
```python
import jax
import jax.numpy as jnp
from jax import lax
from jax.sharding import PartitionSpec as P

EPS = 1e-05


def broadcast(block, axis, holder):
    block = jnp.where(lax.axis_index(axis) == holder, block, jnp.zeros_like(block))
    return lax.psum(block, axis)


def split_up(x, dim, peers):
    dims = x.shape
    tiles = x.reshape(*dims[:dim], peers, dims[dim] // peers, *dims[dim + 1 :])
    return jnp.moveaxis(tiles, dim, 0)


def summed_on_arrival(x, axis, dim):
    peers = lax.axis_size(axis)
    tiles = lax.all_to_all(split_up(x, dim, peers), axis, 0, 0, tiled=True)
    return jnp.sum(tiles.astype(jnp.float32), axis=0)


def together(arrays, axis):
    flat, at, done = (jnp.concatenate([a.reshape(-1) for a in arrays]), 0, [])
    total = lax.psum(flat, axis)
    for a in arrays:
        done.append(total[at : at + a.size].reshape(a.shape))
        at += a.size
    return tuple(done)


def normalize(values):
    center = values - jnp.mean(values, axis=-1, keepdims=True)
    inverse = lax.rsqrt(jnp.mean(center * center, axis=-1, keepdims=True) + EPS)
    return (center * inverse, inverse)


def gating(panel, weight, first_ok, second_ok, hidden):
    projected = jnp.einsum("ikc,ch->ikh", panel, weight, preferred_element_type=jnp.float32)
    values = projected[..., :hidden]
    sigmoid_val = jax.nn.sigmoid(projected[..., hidden:])
    pad_mask = (first_ok[:, None] & second_ok[None, :]).astype(jnp.float32)[..., None]
    return ((pad_mask * sigmoid_val * values).astype(jnp.bfloat16), values, sigmoid_val, pad_mask)


def push_back(partial_value, values, sigmoid_val, pad_mask, weight, panel):
    combined = jnp.concatenate(
        [
            partial_value * pad_mask * sigmoid_val,
            partial_value * pad_mask * values * sigmoid_val * (1.0 - sigmoid_val),
        ],
        axis=-1,
    ).astype(jnp.bfloat16)
    panel_grad = jnp.einsum("ikh,ch->ikc", combined, weight, preferred_element_type=jnp.float32)
    weight_grad = jnp.einsum("ikc,ikh->ch", panel, combined, preferred_element_type=jnp.float32)
    return (panel_grad, weight_grad)


def per_device(
    pair,
    cotangent,
    length,
    norm_gain,
    norm_bias,
    left_weight,
    right_weight,
    gate_weight,
    out_gain,
    out_bias,
    out_weight,
):
    row_index = lax.axis_index("row")
    col_index = lax.axis_index("col")
    n_row = lax.axis_size("row")
    n_col = lax.axis_size("col")
    per_col = n_row // n_col
    rows_dev = pair.shape[0]
    cols_dev = pair.shape[1]
    tokens = rows_dev * n_row
    hidden = out_weight.shape[0]
    pair_hat, pair_scale = normalize(pair.astype(jnp.float32))
    normed = (pair_hat * norm_gain + norm_bias).astype(jnp.bfloat16)
    real_count = length[0]
    second_ok = jnp.arange(tokens, dtype=jnp.int32) < real_count
    own_ok = row_index * rows_dev + jnp.arange(rows_dev, dtype=jnp.int32) < real_count
    partner_ok = col_index * cols_dev + jnp.arange(cols_dev, dtype=jnp.int32) < real_count
    left_tile, left_val, left_sig, tile_mask = gating(
        normed, left_weight, own_ok, partner_ok, hidden
    )
    right_tile, right_val, right_sig, unused_mask = gating(
        normed, right_weight, own_ok, partner_ok, hidden
    )
    row_panel = lax.all_gather(normed, "col", axis=1, tiled=True)
    pieces = []
    for member in range(per_col):
        pieces.append(broadcast(row_panel, "row", col_index * per_col + member))
    col_panel = jnp.concatenate(pieces, axis=0)
    left_act = gating(row_panel, left_weight, own_ok, second_ok, hidden)[0]
    right_act = gating(col_panel, right_weight, partner_ok, second_ok, hidden)[0]
    tri = jnp.einsum("ikh,jkh->ijh", left_act, right_act, preferred_element_type=jnp.float32)
    tri_hat, tri_scale = normalize(tri)
    tri_normed = (tri_hat * out_gain + out_bias).astype(jnp.bfloat16)
    outer_val = jnp.einsum(
        "ijh,hc->ijc", tri_normed, out_weight, preferred_element_type=jnp.float32
    )
    gate_val = jax.nn.sigmoid(
        jnp.einsum("ijc,cd->ijd", normed, gate_weight, preferred_element_type=jnp.float32)
    )
    update = (gate_val * outer_val).astype(jnp.bfloat16)
    upstream = cotangent.astype(jnp.float32)
    outer_grad = (upstream * gate_val).astype(jnp.bfloat16)
    gate_grad = (upstream * outer_val * gate_val * (1.0 - gate_val)).astype(jnp.bfloat16)
    grad_output = jnp.einsum(
        "ijh,ijc->hc", tri_normed, outer_grad, preferred_element_type=jnp.float32
    )
    grad_gating = jnp.einsum("ijc,ijd->cd", normed, gate_grad, preferred_element_type=jnp.float32)
    tnorm_grad = jnp.einsum(
        "ijc,hc->ijh", outer_grad, out_weight, preferred_element_type=jnp.float32
    )
    hat_grad = tnorm_grad * out_gain
    tri_grad = (
        tri_scale
        * (
            hat_grad
            - jnp.mean(hat_grad, axis=-1, keepdims=True)
            - tri_hat * jnp.mean(hat_grad * tri_hat, axis=-1, keepdims=True)
        )
    ).astype(jnp.bfloat16)
    row_partial = jnp.einsum(
        "ijh,jkh->ikh", tri_grad, right_act, preferred_element_type=jnp.float32
    )
    col_partial = jnp.einsum("ijh,ikh->jkh", tri_grad, left_act, preferred_element_type=jnp.float32)
    row_part = summed_on_arrival(row_partial.astype(jnp.bfloat16), "col", 1)
    summed = lax.psum_scatter(
        col_partial.astype(jnp.bfloat16), "row", scatter_dimension=0, tiled=True
    )
    slab = summed[None]
    received = lax.all_to_all(slab, "col", split_axis=2, concat_axis=0, tiled=True)
    select = (jnp.arange(per_col, dtype=jnp.int32) == row_index // n_col).astype(jnp.bfloat16)
    spread = (received[:, None] * select[None, :, None, None, None]).reshape(
        (n_row,) + received.shape[1:]
    )
    returned = lax.all_to_all(spread, "row", split_axis=0, concat_axis=0, tiled=True)
    start = row_index % per_col * n_col
    owned = lax.dynamic_slice_in_dim(returned, start, n_col, 0).reshape(rows_dev, cols_dev, -1)
    col_part = owned.astype(jnp.float32)
    from_rows, grad_left = push_back(row_part, left_val, left_sig, tile_mask, left_weight, normed)
    from_cols, grad_right = push_back(
        col_part, right_val, right_sig, tile_mask, right_weight, normed
    )
    gate_back = jnp.einsum(
        "ijd,cd->ijc", gate_grad, gate_weight, preferred_element_type=jnp.float32
    )
    normed_grad = gate_back + from_rows + from_cols
    scaled = normed_grad * norm_gain
    grad_pair = (
        pair_scale
        * (
            scaled
            - jnp.mean(scaled, axis=-1, keepdims=True)
            - pair_hat * jnp.mean(scaled * pair_hat, axis=-1, keepdims=True)
        )
    ).astype(jnp.bfloat16)
    grad_norms = jnp.stack(
        [
            jnp.sum(normed_grad * pair_hat, axis=(0, 1)),
            jnp.sum(normed_grad, axis=(0, 1)),
            jnp.sum(tnorm_grad * tri_hat, axis=(0, 1)),
            jnp.sum(tnorm_grad, axis=(0, 1)),
        ]
    )
    totals = together((grad_left, grad_right, grad_gating, grad_output, grad_norms), ("row", "col"))
    inverse = 1.0 / tokens
    return (
        update,
        grad_pair,
        totals[0] * inverse,
        totals[1] * inverse,
        totals[2] * inverse,
        totals[3] * inverse,
        totals[4] * inverse,
    )


def solution(mesh):
    return jax.shard_map(
        per_device,
        mesh=mesh,
        in_specs=(
            P("row", "col", None),
            P("row", "col", None),
            P(),
            P(),
            P(),
            P(),
            P(),
            P(),
            P(),
            P(),
            P(),
        ),
        out_specs=(P("row", "col", None), P("row", "col", None), P(), P(), P(), P(), P()),
        check_vma=False,
    )
```

profile of v0, /device:TPU:0, one launch (start us, length us, event | category | flops | bytes accessed | tf_op | source)
XLA Modules:
  0.0 730.8 jit_solution(15539498948825562416)
XLA Ops:
  7.2 1.4 convert_reduce_fusion.1
  8.6 1.7 fusion.33
  10.3 2.5 fusion.27
  12.9 92.3 %all-gather.2.cloned.1.call-done = bf16[32,512,128]{2,1,0:T(8,128)(2,1)} async-done(((bf16[32,64,128]{2,1,0:T(8,128)(2,1)}), bf16[32,512,128]{2,1,0:T(8,128)(2,1)}) %all-gather.2.cloned.1.call-update) | async-done | bytes 4194320 | tf_op jit(solution)/shard_map/all_gather | solution.py:96
  105.2 5.9 broadcast_select_fusion.1
  112.6 1.4 fusion.78
  114.0 3.1 copy.55
  117.3 4.5 fusion.57
  121.8 4.4 fusion.5
  126.2 8.0 %copy.53 = bf16[32,512,128]{1,0,2:T(8,128)(2,1)} copy(bf16[32,512,128]{2,1,0:T(8,128)(2,1)} %fusion.5) | data formatting | bytes 8388608 | tf_op jit(solution)/shard_map/convert_element_type | solution.py:46
  134.2 141.9 %all-reduce.6.cloned.1.call-done = (bf16[32,512,128]{2,1,0:T(8,128)(2,1)}, bf16[32,512,128]{2,1,0:T(8,128)(2,1)}) async-done(((bf16[32,512,128]{2,1,0:T(8,128)(2,1)}, bf16[32,512,128]{2,1,0:T(8,128)(2,1)}), (bf16[32,512,128]{2,1,0:T(8,128)(2,1)}, bf16[32,512,128]{2,1,0:T(8,128)(2,1)})) %all-reduce.6.cloned.1.call-update) | async-done | bytes 8388624 | tf_op jit(solution)/shard_map/psum | solution.py:11
  276.1 19.0 %fusion.10 = f32[64,512,256]{2,1,0:T(8,128)} fusion(bf16[32,512,128]{2,1,0:T(8,128)(2,1)} %get-tuple-element.14, bf16[32,512,128]{2,1,0:T(8,128)(2,1)} %get-tuple-element.15, bf16[128,256]{1,0:T(8,128)(2,1)S(1)} %copy-done), kind=kOutput, calls=%fused_computation.14 | convolution fusion | flops 2151677952 | bytes 42008576 | tf_op jit(solution)/shard_map/ikc,ch->ikh/dot_general | solution.py:42
  295.1 16.2 %fusion = bf16[64,512,128]{2,1,0:T(8,128)(2,1)} fusion(f32[64,512,256]{2,1,0:T(8,128)} %fusion.10, f32[64,512]{1,0:T(8,128)S(1)} %and_convert_fusion), kind=kLoop, calls=%fused_computation.1 | loop fusion | flops 25165824 | bytes 42074112 | tf_op jit(solution)/shard_map/convert_element_type | solution.py:46
  311.4 12.5 %copy.52 = bf16[64,512,128]{1,0,2:T(8,128)(2,1)} copy(bf16[64,512,128]{2,1,0:T(8,128)(2,1)} %fusion) | data formatting | bytes 16777216 | tf_op jit(solution)/shard_map/convert_element_type | solution.py:46
  323.9 6.9 bitcast_reduce_fusion
  331.2 1.3 multiply_reduce_fusion
  332.5 1.9 multiply_convert_fusion
  334.3 1.0 copy-done.2
  335.3 5.6 convert_bitcast_fusion
  340.9 13.0 %copy.60 = bf16[64,512,128]{2,1,0:T(8,128)(2,1)} copy(bf16[64,512,128]{1,0,2:T(8,128)(2,1)} %convert_bitcast_fusion) | data formatting | bytes 16777216 | tf_op jit(solution)/shard_map/convert_element_type | solution.py:138
  353.9 102.8 %reduce-scatter.2.cloned.1.call-done = bf16[4,512,128]{2,1,0:T(8,128)(2,1)} async-done(((bf16[64,512,128]{2,1,0:T(8,128)(2,1)}), bf16[4,512,128]{2,1,0:T(8,128)(2,1)}) %reduce-scatter.2.cloned.1.call-update) | async-done | bytes 524304 | tf_op jit(solution)/shard_map/reduce_scatter | solution.py:137
  456.7 2.2 copy.61
  459.0 4.4 all-to-all-start.1
  463.3 6.6 convert_bitcast_fusion.1
  470.0 7.9 %copy.57 = bf16[32,512,128]{2,1,0:T(8,128)(2,1)} copy(bf16[32,512,128]{1,0,2:T(8,128)(2,1)} %convert_bitcast_fusion.1) | data formatting | bytes 8388608 | tf_op jit(solution)/shard_map/convert_element_type | solution.py:136
  477.8 5.5 copy.58
  483.3 5.8 all-to-all-start
  489.3 1.7 fusion.55
  491.0 1.8 fusion.60
  492.9 1.4 bitcast_multiply_fusion
  494.3 52.4 %all-to-all-done = bf16[8,32,64,128]{3,2,1,0:T(8,128)(2,1)} async-done(((bf16[8,32,64,128]{3,2,1,0:T(8,128)(2,1)}), bf16[8,32,64,128]{3,2,1,0:T(8,128)(2,1)}, u32[]{:S(2)}, u32[]{:S(2)}) %all-to-all-start) | async-done | bytes 4194336 | tf_op jit(solution)/shard_map/all_to_all | solution.py:22
  546.7 5.0 all-to-all-start.2
  552.1 2.2 copy.54
  554.3 1.2 fusion.36
  555.5 0.8 copy-done.10
  556.3 1.3 fusion.67
  557.6 4.1 convert_reduce_fusion
  561.7 8.0 %all-to-all-done.2 = bf16[16,4,64,128]{3,2,1,0:T(8,128)(2,1)} async-done(((bf16[16,4,64,128]{3,2,1,0:T(8,128)(2,1)}), bf16[16,4,64,128]{3,2,1,0:T(8,128)(2,1)}, u32[]{:S(2)}, u32[]{:S(2)}) %all-to-all-start.2) | async-done | bytes 1048608 | tf_op jit(solution)/shard_map/all_to_all | solution.py:146
  569.7 1.1 constant_dynamic-slice_fusion
  570.8 3.0 fusion.51
  576.1 1.0 fusion.15
  577.1 1.0 fusion.14
  578.5 1.2 fusion.32
  580.3 2.0 fusion.31
  582.3 136.8 %all-reduce.4.cloned.1.call-done = f32[98816]{0:T(1024)} async-done(((f32[98816]{0:T(1024)}), f32[98816]{0:T(1024)}) %all-reduce.4.cloned.1.call-update) | async-done | bytes 395280 | tf_op jit(solution)/shard_map/psum | solution.py:28
  719.1 1.0 slice_multiply_fusion.4
  721.5 1.5 fusion.52
  723.0 1.3 fusion.70
  (72 shorter events, 6.6 us)
Async XLA Ops:
  7.2 268.9 %copy-start = (bf16[128,256]{1,0:T(8,128)(2,1)S(1)}, bf16[128,256]{1,0:T(8,128)(2,1)}, u32[]{:S(2)}) copy-start(bf16[128,256]{1,0:T(8,128)(2,1)} %param.17) | copy-start | bytes 196612
  7.2 98.0 %all-gather.2.cloned.1.call-start = ((), (), s32[]{:S(2)}) async-start(), calls=%async_computation.4 | async-start | bytes 4718592 | tf_op jit(solution)/shard_map/all_gather | solution.py:96
  12.8 263.3 %all-reduce.6.cloned.1.call-start = ((), (), s32[]{:S(2)}) async-start(), calls=%async_computation.7 | async-start | bytes 16777216 | tf_op jit(solution)/shard_map/psum | solution.py:11
  111.1 1.0 copy-start.5
  111.1 1.0 copy-start.14
  111.2 1.4 copy-start.7
  111.2 1.4 copy-start.13
  111.2 345.5 %reduce-scatter.2.cloned.1.call-start = ((), (), s32[]{:S(2)}) async-start(), calls=%async_computation.5 | async-start | bytes 8912896 | tf_op jit(solution)/shard_map/reduce_scatter | solution.py:137
  112.2 5.1 copy-start.12
  323.9 7.3 copy-start.16
  330.8 1.7 copy-start.17
  332.4 2.9 copy-start.1
  334.3 1.0 copy-start.2
  353.9 109.5 %copy-start.3 = (bf16[32,64,128]{1,0,2:T(8,128)(2,1)S(1)}, bf16[32,64,128]{1,0,2:T(8,128)(2,1)}, u32[]{:S(2)}) copy-start(bf16[32,64,128]{1,0,2:T(8,128)(2,1)} %copy-done.2) | copy-start | bytes 1572868
  459.0 24.4 %all-to-all-start.1 = ((bf16[1,4,512,128]{3,1,0,2:T(4,128)(2,1)}), bf16[1,4,512,128]{3,1,0,2:T(4,128)(2,1)S(1)}, u32[]{:S(2)}, u32[]{:S(2)}) async-start(bf16[1,4,512,128]{3,1,0,2:T(4,128)(2,1)} %copy.61), calls=%async_computation.2 | async-start | bytes 1048576 | tf_op jit(solution)/shard_map/all_to_all | solution.py:141
  483.3 5.9 copy-start.6
  483.3 63.4 %all-to-all-start = ((bf16[8,32,64,128]{3,2,1,0:T(8,128)(2,1)}), bf16[8,32,64,128]{3,2,1,0:T(8,128)(2,1)}, u32[]{:S(2)}, u32[]{:S(2)}) async-start(bf16[8,32,64,128]{3,2,1,0:T(8,128)(2,1)} %copy.58), calls=%async_computation | async-start | bytes 8388608 | tf_op jit(solution)/shard_map/all_to_all | solution.py:22
  491.0 63.3 %copy-start.8 = (bf16[32,64,128]{2,1,0:T(8,128)(2,1)S(1)}, bf16[32,64,128]{2,1,0:T(8,128)(2,1)}, u32[]{:S(2)}) copy-start(bf16[32,64,128]{2,1,0:T(8,128)(2,1)} %param.12) | copy-start | bytes 1572868
  546.7 23.0 %all-to-all-start.2 = ((bf16[16,4,64,128]{3,2,1,0:T(8,128)(2,1)}), bf16[16,4,64,128]{3,2,1,0:T(8,128)(2,1)}, u32[]{:S(2)}, u32[]{:S(2)}) async-start(bf16[16,4,64,128]{3,2,1,0:T(8,128)(2,1)} %bitcast_multiply_fusion), calls=%async_computation.3 | async-start | bytes 2097152 | tf_op jit(solution)/shard_map/all_to_all | solution.py:146
  551.7 167.4 %all-reduce.4.cloned.1.call-start = ((), (), s32[]{:S(2)}) async-start(), calls=%async_computation.6 | async-start | bytes 794624 | tf_op jit(solution)/shard_map/psum | solution.py:28
  555.5 0.8 copy-start.10
  573.8 2.2 copy-start.11
  573.9 4.2 copy-start.9
  574.3 4.2 copy-start.4
  574.3 4.2 copy-start.15
Sparse Core Ops, SparseCore 0:
  12.9 92.2 all-gather.1
  111.3 164.7 all-reduce.5
  354.0 102.6 reduce-scatter.1
  580.4 138.6 all-reduce.3
where the time goes:
time: 733 us; the launch traced here: 731 us
  waiting for transfers between devices  534 us (73%)
  local copies, waits for them, and re-layouts  60.6 us (8%)
  matrix products  54.7 us (7%)
  other arithmetic  50.7 us (7%)
  starting transfers between devices  15.6 us (2%)
  between operations  14.8 us (2%)
    psum x1, waiting for transfers between devices, broadcast(): return lax.psum(block, axis)  142 us
    psum x1, waiting for transfers between devices, together(): total = lax.psum(flat, axis)  137 us
    reduce_scatter x1, waiting for transfers between devices, per_device(): lax.psum_scatter(col_partial.astype(jnp.bfloat16), 'row', scatter_dimensi...  103 us
    all_gather x1, waiting for transfers between devices, per_device(): row_panel = lax.all_gather(normed, 'col', axis=1, tiled=True)  92.3 us
    all_to_all x1, waiting for transfers between devices, summed_on_arrival(): tiles = lax.all_to_all(split_up(x, dim, peers), axis, 0, 0, tiled=True)  52.4 us
    dot_general x4, matrix products, gating(): jnp.einsum('ikc,ch->ikh', panel, weight, preferred_element_type=jnp.float32)  27.1 us
    convert_element_type x2, other arithmetic, gating(): (pad_mask * sigmoid_val * values).astype(jnp.bfloat16)  20.6 us
    convert_element_type x2, local copies, waits for them, and re-layouts, gating(): (pad_mask * sigmoid_val * values).astype(jnp.bfloat16)  20.5 us
  transfers between devices with their start and end apart: 7, of which 6 were waited for; matrix products, arithmetic and copies ran while one was open for 8% of the time, Pallas kernels for 0%

commit v1 on v0

v1 whole, which is shorter than its diff:
```python
import jax
import jax.numpy as jnp
from jax import lax
from jax.sharding import PartitionSpec as P

EPS = 1e-05
AXES = ("row", "col")


def normalize(values):
    center = values - jnp.mean(values, axis=-1, keepdims=True)
    inverse = lax.rsqrt(jnp.mean(center * center, axis=-1, keepdims=True) + EPS)
    return (center * inverse, inverse)


def exchange(x):
    return lax.all_to_all(x, AXES, 0, 0, tiled=True)


def per_device(
    pair,
    cotangent,
    length,
    norm_gain,
    norm_bias,
    left_weight,
    right_weight,
    gate_weight,
    out_gain,
    out_bias,
    out_weight,
):
    n_row = lax.axis_size("row")
    n_col = lax.axis_size("col")
    n = n_row * n_col
    rows, cols = pair.shape[:2]
    tokens = rows * n_row
    hidden = out_weight.shape[0]
    row_at = lax.axis_index("row") * rows
    col_at = lax.axis_index("col") * cols
    first_ok = row_at + jnp.arange(rows, dtype=jnp.int32) < length[0]
    second_ok = col_at + jnp.arange(cols, dtype=jnp.int32) < length[0]
    mask = (first_ok[:, None] & second_ok[None, :]).astype(jnp.float32).reshape(1, -1)

    def to_owner(tiles):
        return exchange(jnp.stack([t.reshape(n, rows * cols // 128, 128) for t in tiles], axis=1))

    def whole(received):
        return received.reshape(n_row, n_col, rows, cols).transpose(0, 2, 1, 3).reshape(tokens, tokens)

    def tiled(matrix):
        t = matrix.reshape(n_row, rows, n_col, cols).transpose(0, 2, 1, 3)
        return t.reshape(n, rows * cols // 128, 128)

    pair_hat, pair_scale = normalize(pair.astype(jnp.float32))
    normed = (pair_hat * norm_gain + norm_bias).astype(jnp.bfloat16)
    flat = normed.reshape(rows * cols, -1)

    def dot(form, a, b):
        return jnp.einsum(form, a, b, preferred_element_type=jnp.float32)

    def gating(weight):
        projected = dot("pc,ch->hp", flat, weight)
        values = projected[:hidden]
        sig = jax.nn.sigmoid(projected[hidden:])
        return (mask * sig * values).astype(jnp.bfloat16), values, sig

    left, left_val, left_sig = gating(left_weight)
    right, right_val, right_sig = gating(right_weight)
    got = to_owner([left, right])
    big_l = whole(got[:, 0])
    big_r = whole(got[:, 1])
    tri_own = dot("ik,jk->ij", big_l, big_r).astype(jnp.bfloat16)
    tri = exchange(tiled(tri_own)).reshape(hidden, -1).astype(jnp.float32)
    center = tri - jnp.mean(tri, axis=0, keepdims=True)
    tri_scale = lax.rsqrt(jnp.mean(center * center, axis=0, keepdims=True) + EPS)
    tri_hat = center * tri_scale
    tri_normed = (tri_hat * out_gain[:, None] + out_bias[:, None]).astype(jnp.bfloat16)
    outer = dot("hp,hc->cp", tri_normed, out_weight)
    gate = jax.nn.sigmoid(dot("pc,cd->dp", flat, gate_weight))
    update = (gate * outer).astype(jnp.bfloat16).T.reshape(pair.shape)
    upstream = cotangent.reshape(rows * cols, -1).T.astype(jnp.float32)
    outer_grad = (upstream * gate).astype(jnp.bfloat16)
    gate_grad = (upstream * outer * gate * (1.0 - gate)).astype(jnp.bfloat16)
    grad_output = dot("hp,cp->hc", tri_normed, outer_grad)
    grad_gating = dot("pc,dp->cd", flat, gate_grad)
    tnorm_grad = dot("cp,hc->hp", outer_grad, out_weight)
    hat_grad = tnorm_grad * out_gain[:, None]
    tri_grad = (
        tri_scale
        * (
            hat_grad
            - jnp.mean(hat_grad, axis=0, keepdims=True)
            - tri_hat * jnp.mean(hat_grad * tri_hat, axis=0, keepdims=True)
        )
    ).astype(jnp.bfloat16)
    g = whole(exchange(tri_grad.reshape(n, rows * cols // 128, 128)))
    row_own = dot("ij,jk->ik", g, big_r).astype(jnp.bfloat16)
    col_own = dot("ij,ik->jk", g, big_l).astype(jnp.bfloat16)
    back = exchange(jnp.stack([tiled(row_own), tiled(col_own)], axis=1))
    row_part = back[:, 0].reshape(hidden, -1).astype(jnp.float32)
    col_part = back[:, 1].reshape(hidden, -1).astype(jnp.float32)

    def push_back(part, values, sig, weight):
        comb = jnp.concatenate(
            [part * mask * sig, part * mask * values * sig * (1.0 - sig)], axis=0
        ).astype(jnp.bfloat16)
        return dot("hp,ch->pc", comb, weight), dot("pc,hp->ch", flat, comb)

    from_rows, grad_left = push_back(row_part, left_val, left_sig, left_weight)
    from_cols, grad_right = push_back(col_part, right_val, right_sig, right_weight)
    gate_back = dot("dp,cd->pc", gate_grad, gate_weight)
    normed_grad = (gate_back + from_rows + from_cols).reshape(pair.shape)
    scaled = normed_grad * norm_gain
    grad_pair = (
        pair_scale
        * (
            scaled
            - jnp.mean(scaled, axis=-1, keepdims=True)
            - pair_hat * jnp.mean(scaled * pair_hat, axis=-1, keepdims=True)
        )
    ).astype(jnp.bfloat16)
    grad_norms = jnp.stack(
        [
            jnp.sum(normed_grad * pair_hat, axis=(0, 1)),
            jnp.sum(normed_grad, axis=(0, 1)),
            jnp.sum(tnorm_grad * tri_hat, axis=1),
            jnp.sum(tnorm_grad, axis=1),
        ]
    )
    parts = [grad_left, grad_right, grad_gating, grad_output, grad_norms]
    flat_parts = jnp.concatenate([a.reshape(-1, 128) for a in parts], axis=0)
    size = flat_parts.shape[0]
    per = -(-size // (n * 8)) * 8
    padded = jnp.pad(flat_parts, ((0, per * n - size), (0, 0))).reshape(n, per, 128)
    mine = jnp.sum(exchange(padded), axis=0) * (1.0 / tokens)
    total = lax.all_gather(mine, AXES, axis=0, tiled=True)
    done, at = [], 0
    for a in parts:
        count = a.size // 128
        done.append(total[at : at + count].reshape(a.shape))
        at += count
    return (update, grad_pair, *done)


def solution(mesh):
    return jax.shard_map(
        per_device,
        mesh=mesh,
        in_specs=(P("row", "col", None), P("row", "col", None)) + (P(),) * 9,
        out_specs=(P("row", "col", None), P("row", "col", None)) + (P(),) * 5,
        check_vma=False,
    )
```

time: 733 us -> 507 us (0.69)
  waiting for transfers between devices: 534 us -> 24.6 us
  blocking collectives: 0 us -> 380 us
  matrix products: 54.7 us -> 18 us
  other arithmetic: 50.7 us -> 20.7 us
  between operations: 14.8 us -> 1.83 us
  local copies, waits for them, and re-layouts: 60.6 us -> 48.8 us
    all_gather x0 -> x1, blocking collectives: none -> 314 us  [per_device(): total = lax.all_gather(mine, AXES, axis=0, tiled=True)]
    psum x2 -> x0, waiting for transfers between devices: 279 us -> none  [the longest x1 142 us: broadcast(): return lax.psum(block, axis)]
    reduce_scatter x1 -> x0, waiting for transfers between devices: 103 us -> none  [per_device(): lax.psum_scatter(col_partial.astype(jnp.bfloat16), 'row', scatter_dimensi...]
    all_gather x1 -> x0, waiting for transfers between devices: 92.3 us -> none  [per_device(): row_panel = lax.all_gather(normed, 'col', axis=1, tiled=True)]
    all_to_all x0 -> x3, blocking collectives: none -> 66.2 us  [exchange(): return lax.all_to_all(x, AXES, 0, 0, tiled=True)]
    convert_element_type x5 -> x4, local copies, waits for them, and re-layouts: 43.6 us -> 5.68 us  [the longest x1 2.56 us: per_device(): col_part = back[:, 1].reshape(hidden, -1).astype(jnp.float32)]
    dot_general x17 -> x15, matrix products: 54.7 us -> 18 us  [dot(): return jnp.einsum(form, a, b, preferred_element_type=jnp.float32)]
    all_to_all x3 -> x2, waiting for transfers between devices: 60.4 us -> 24.6 us  [exchange(): return lax.all_to_all(x, AXES, 0, 0, tiled=True)]
  transfers between devices with their start and end apart: 7 -> 2, of which waited for: 6 -> 2; matrix products, arithmetic and copies ran while one was open for 8% -> 1% of each run, Pallas kernels for 0% -> 0%
where the time goes in v1:
time: 507 us; the launch traced here: 505 us
  blocking collectives  380 us (75%)
  local copies, waits for them, and re-layouts  48.8 us (10%)
  waiting for transfers between devices  24.6 us (5%)
  other arithmetic  20.7 us (4%)
  matrix products  18 us (4%)
  starting transfers between devices  11.3 us (2%)
    all_gather x1, blocking collectives, per_device(): total = lax.all_gather(mine, AXES, axis=0, tiled=True)  314 us
    all_to_all x3, blocking collectives, exchange(): return lax.all_to_all(x, AXES, 0, 0, tiled=True)  66.2 us
    all_to_all x2, waiting for transfers between devices, exchange(): return lax.all_to_all(x, AXES, 0, 0, tiled=True)  24.6 us
    dot_general x15, matrix products, dot(): return jnp.einsum(form, a, b, preferred_element_type=jnp.float32)  18 us
    all_to_all x2, starting transfers between devices, exchange(): return lax.all_to_all(x, AXES, 0, 0, tiled=True)  11.3 us
  transfers between devices with their start and end apart: 2, of which 2 were waited for; matrix products, arithmetic and copies ran while one was open for 1% of the time, Pallas kernels for 0%

profile of v1, /device:TPU:0, one launch (start us, length us, event | category | flops | bytes accessed | tf_op | source)
XLA Modules:
  0.0 505.4 jit_solution(2819725478493641133)
XLA Ops:
  1.5 1.4 convert_reduce_fusion
  2.9 1.7 fusion.17
  4.7 1.7 fusion.11
  8.9 1.2 copy.32
  11.7 29.5 %all_to_all.25 = bf16[128,2,16,128]{3,2,1,0:T(8,128)(2,1)S(1)} all-to-all(bf16[128,2,16,128]{3,2,1,0:T(8,128)(2,1)S(1)} %pad_maximum_fusion), channel_id=1, replica_groups=mesh['row'=16,'col'=8] {'row','col'}, dimensions={0} | all-to-all | bytes 2097152 | tf_op jit(solution)/shard_map/all_to_all | solution.py:17
  42.3 1.6 reshape_squeeze.9
  44.0 1.4 copy.35
  45.4 1.9 reshape.175
  47.3 2.6 reshape_squeeze.8
  49.9 2.7 copy.34
  52.6 1.9 reshape.174
  55.3 1.3 convolution_convert_fusion.2
  56.5 1.6 reshape.176
  58.2 1.2 copy.50
  59.4 1.8 reshape.177
  61.2 18.5 %all_to_all.26 = bf16[128,16,128]{2,1,0:T(8,128)(2,1)S(1)} all-to-all(bf16[128,16,128]{2,1,0:T(8,128)(2,1)S(1)} %reshape.177), channel_id=1, replica_groups=mesh['row'=16,'col'=8] {'row','col'}, dimensions={0} | all-to-all | bytes 1048576 | tf_op jit(solution)/shard_map/all_to_all | solution.py:17
  80.5 1.5 copy.37
  83.0 1.2 multiply_convert_fusion.5
  85.4 1.7 fusion.24
  87.1 2.4 multiply_convert_fusion.4
  89.4 1.5 copy.38
  90.9 18.2 %all_to_all.27 = bf16[128,16,128]{2,1,0:T(8,128)(2,1)} all-to-all(bf16[128,16,128]{2,1,0:T(8,128)(2,1)S(1)} %copy.38), channel_id=1, replica_groups=mesh['row'=16,'col'=8] {'row','col'}, dimensions={0} | all-to-all | bytes 1048576 | tf_op jit(solution)/shard_map/all_to_all | solution.py:17
  109.1 1.6 reshape.180
  110.8 1.4 copy.39
  112.2 1.9 reshape.181
  114.2 2.3 convolution_convert_fusion
  116.5 1.2 convolution_convert_fusion.1
  117.7 1.6 reshape.182
  119.3 1.2 copy.49
  120.5 2.4 stack_reshape.14
  123.0 1.6 reshape.183
  124.6 1.2 copy.48
  125.8 1.8 stack_reshape.15
  128.8 1.2 copy.42
  129.9 6.0 %all-to-all-start.3 = ((bf16[128,2,16,128]{3,2,1,0:T(8,128)(2,1)}), bf16[128,2,16,128]{3,2,1,0:T(8,128)(2,1)}, u32[]{:S(2)}, u32[]{:S(2)}) async-start(bf16[128,2,16,128]{3,2,1,0:T(8,128)(2,1)} %copy.42), calls=%async_computation.3 | async-start | bytes 2097152 | tf_op jit(solution)/shard_map/all_to_all | solution.py:17
  136.2 2.2 fusion.48
  138.4 2.2 fusion.47
  140.5 13.3 %all-to-all-done.3 = bf16[128,2,16,128]{3,2,1,0:T(8,128)(2,1)} async-done(((bf16[128,2,16,128]{3,2,1,0:T(8,128)(2,1)}), bf16[128,2,16,128]{3,2,1,0:T(8,128)(2,1)}, u32[]{:S(2)}, u32[]{:S(2)}) %all-to-all-start.3) | async-done | bytes 1048608 | tf_op jit(solution)/shard_map/all_to_all | solution.py:17
  153.8 2.7 slice_convert_fusion.1
  156.5 1.6 copy.43
  158.1 2.6 copy.44
  160.6 2.4 multiply_convert_fusion.3
  164.2 1.4 fusion.36
  165.7 2.3 fusion.42
  170.0 5.3 %all-to-all-start.4 = ((f32[128,8,128]{2,1,0:T(8,128)}), f32[128,8,128]{2,1,0:T(8,128)S(1)}, u32[]{:S(2)}, u32[]{:S(2)}) async-start(f32[128,8,128]{2,1,0:T(8,128)} %pad_bitcast_fusion), calls=%async_computation.4 | async-start | bytes 1048576 | tf_op jit(solution)/shard_map/all_to_all | solution.py:17
  175.4 1.9 fusion.15
  177.3 11.4 %all-to-all-done.4 = f32[128,8,128]{2,1,0:T(8,128)S(1)} async-done(((f32[128,8,128]{2,1,0:T(8,128)}), f32[128,8,128]{2,1,0:T(8,128)S(1)}, u32[]{:S(2)}, u32[]{:S(2)}) %all-to-all-start.4) | async-done | bytes 524320 | tf_op jit(solution)/shard_map/all_to_all | solution.py:17
  188.8 313.9 %all_gather.3 = f32[1024,128]{1,0:T(8,128)S(1)} all-gather(f32[8,128]{1,0:T(8,128)S(1)} %broadcast_multiply_fusion.6), channel_id=1, replica_groups=mesh['row'=16,'col'=8] {'row','col'}, dimensions={0}, use_global_device_ids=true | all-gather | bytes 528384 | tf_op jit(solution)/shard_map/all_gather | solution.py:137
  (92 shorter events, 16.5 us)
Async XLA Ops:
  0.6 5.7 %copy-start = (bf16[128,256]{1,0:T(8,128)(2,1)S(1)}, bf16[128,256]{1,0:T(8,128)(2,1)}, u32[]{:S(2)}) copy-start(bf16[128,256]{1,0:T(8,128)(2,1)} %param.17) | copy-start | bytes 196612
  2.9 4.2 copy-start.18
  6.3 0.8 copy-start.6
  7.6 1.3 copy-start.1
  47.3 7.2 %copy-start.9 = (bf16[512,512]{1,0:T(8,128)(2,1)}, bf16[512,512]{1,0:T(8,128)(2,1)S(1)}, u32[]{:S(2)}) copy-start(bf16[512,512]{1,0:T(8,128)(2,1)S(1)} %reshape.175) | copy-start | bytes 1572868
  54.5 0.8 copy-start.14
  61.2 20.8 %copy-start.22 = (f32[128]{0:T(128)S(1)}, f32[128]{0:T(128)}, u32[]{:S(2)}) copy-start(f32[128]{0:T(128)} %param.19) | copy-start | bytes 1540
  61.2 20.8 %copy-start.25 = (f32[128]{0:T(128)S(1)}, f32[128]{0:T(128)}, u32[]{:S(2)}) copy-start(f32[128]{0:T(128)} %param.20) | copy-start | bytes 1540
  79.7 0.8 copy-start.5
  79.7 2.9 copy-start.19
  80.5 2.4 copy-start.20
  82.0 1.0 copy-start.7
  82.6 1.6 copy-start.13
  83.0 1.2 copy-start.15
  85.4 4.1 copy-start.11
  87.0 2.4 copy-start.3
  112.2 4.3 copy-start.10
  128.8 7.1 %copy-start.4 = (f32[2048,128]{1,0:T(8,128)S(1)}, f32[2048,128]{1,0:T(8,128)}, u32[]{:S(2)}) copy-start(f32[2048,128]{1,0:T(8,128)} %copy-done.3) | copy-start | bytes 3145732
  129.9 23.9 %all-to-all-start.3 = ((bf16[128,2,16,128]{3,2,1,0:T(8,128)(2,1)}), bf16[128,2,16,128]{3,2,1,0:T(8,128)(2,1)}, u32[]{:S(2)}, u32[]{:S(2)}) async-start(bf16[128,2,16,128]{3,2,1,0:T(8,128)(2,1)} %copy.42), calls=%async_computation.3 | async-start | bytes 2097152 | tf_op jit(solution)/shard_map/all_to_all | solution.py:17
  160.6 2.4 copy-start.8
  163.9 1.8 copy-start.12
  163.9 1.8 copy-start.21
  165.6 2.4 copy-start.2
  168.0 1.1 copy-start.16
  168.0 1.1 copy-start.17
  168.0 1.1 copy-start.23
  168.0 1.1 copy-start.24
  170.0 18.7 %all-to-all-start.4 = ((f32[128,8,128]{2,1,0:T(8,128)}), f32[128,8,128]{2,1,0:T(8,128)S(1)}, u32[]{:S(2)}, u32[]{:S(2)}) async-start(f32[128,8,128]{2,1,0:T(8,128)} %pad_bitcast_fusion), calls=%async_computation.4 | async-start | bytes 1048576 | tf_op jit(solution)/shard_map/all_to_all | solution.py:17

commit v2 on v1

--- a/solution.py
+++ b/solution.py
@@ -134,7 +134,7 @@
     per = -(-size // (n * 8)) * 8
     padded = jnp.pad(flat_parts, ((0, per * n - size), (0, 0))).reshape(n, per, 128)
     mine = jnp.sum(exchange(padded), axis=0) * (1.0 / tokens)
-    total = lax.all_gather(mine, AXES, axis=0, tiled=True)
+    total = exchange(jnp.broadcast_to(mine[None], (n,) + mine.shape)).reshape(n * per, 128)
     done, at = [], 0
     for a in parts:
         count = a.size // 128

time: 507 us -> 211 us (0.42)
  blocking collectives: 380 us -> 84.7 us
    all_gather x1 -> x0, blocking collectives: 314 us -> none  [per_device(): total = lax.all_gather(mine, AXES, axis=0, tiled=True)]
    all_to_all x3 -> x4, blocking collectives: 66.2 us -> 84.7 us  [exchange(): return lax.all_to_all(x, AXES, 0, 0, tiled=True)]
  transfers between devices with their start and end apart: 2 -> 2, of which waited for: 2 -> 2; matrix products, arithmetic and copies ran while one was open for 1% -> 3% of each run, Pallas kernels for 0% -> 0%
where the time goes in v2:
time: 211 us; the launch traced here: 210 us
  blocking collectives  84.7 us (40%)
  local copies, waits for them, and re-layouts  48.9 us (23%)
  waiting for transfers between devices  24.6 us (12%)
  other arithmetic  20.7 us (10%)
  matrix products  18 us (9%)
  starting transfers between devices  10.9 us (5%)
    all_to_all x4, blocking collectives, exchange(): return lax.all_to_all(x, AXES, 0, 0, tiled=True)  84.7 us
    all_to_all x2, waiting for transfers between devices, exchange(): return lax.all_to_all(x, AXES, 0, 0, tiled=True)  24.6 us
    dot_general x15, matrix products, dot(): return jnp.einsum(form, a, b, preferred_element_type=jnp.float32)  18 us
    all_to_all x2, starting transfers between devices, exchange(): return lax.all_to_all(x, AXES, 0, 0, tiled=True)  10.9 us
    reshape x6, local copies, waits for them, and re-layouts, tiled(): t = matrix.reshape(n_row, rows, n_col, cols).transpose(0, 2, 1, 3)  8.55 us
    reshape x4, local copies, waits for them, and re-layouts, whole(): received.reshape(n_row, n_col, rows, cols).transpose(0, 2, 1, 3)  7.37 us
    transpose x3, local copies, waits for them, and re-layouts, whole(): received.reshape(n_row, n_col, rows, cols).transpose(0, 2, 1, 3)  5.51 us
    another operation x3, local copies, waits for them, and re-layouts, per_device(): back = exchange(jnp.stack([tiled(row_own), tiled(col_own)], axis=1))  5.38 us
  transfers between devices with their start and end apart: 2, of which 2 were waited for; matrix products, arithmetic and copies ran while one was open for 3% of the time, Pallas kernels for 0%

profile of v2, /device:TPU:0, one launch (start us, length us, event | category | flops | bytes accessed | tf_op | source)
XLA Modules:
  0.0 209.6 jit_solution(9787341782227586618)
XLA Ops:
  1.5 1.4 convert_reduce_fusion
  2.9 1.7 fusion.17
  4.7 1.7 fusion.11
  8.9 1.2 copy.32
  11.7 29.5 %all_to_all.30 = bf16[128,2,16,128]{3,2,1,0:T(8,128)(2,1)S(1)} all-to-all(bf16[128,2,16,128]{3,2,1,0:T(8,128)(2,1)S(1)} %pad_maximum_fusion), channel_id=1, replica_groups=mesh['row'=16,'col'=8] {'row','col'}, dimensions={0} | all-to-all | bytes 2097152 | tf_op jit(solution)/shard_map/all_to_all | solution.py:17
  42.3 1.6 reshape_squeeze.9
  44.0 1.4 copy.35
  45.4 1.9 reshape.187
  47.3 2.6 %reshape_squeeze.8 = bf16[16,8,32,64]{3,2,1,0:T(8,128)(2,1)} reshape(bf16[128,1,16,128]{3,2,1,0:T(8,128)(2,1)} %get-tuple-element.23) | data formatting | bytes 1048576 | tf_op jit(solution)/shard_map/reshape;squeeze | solution.py:49
  49.9 2.7 %copy.34 = bf16[16,32,8,64]{3,2,1,0:T(8,128)(2,1)} copy(bf16[16,32,8,64]{3,1,2,0:T(8,128)(2,1)} %bitcast.153) | data formatting | bytes 1048576 | tf_op jit(solution)/shard_map/transpose | solution.py:49
  52.6 1.9 reshape.186
  55.3 1.3 convolution_convert_fusion.2
  56.5 1.6 reshape.188
  58.2 1.2 copy.50
  59.4 1.8 reshape.189
  61.2 18.5 %all_to_all.31 = bf16[128,16,128]{2,1,0:T(8,128)(2,1)S(1)} all-to-all(bf16[128,16,128]{2,1,0:T(8,128)(2,1)S(1)} %reshape.189), channel_id=1, replica_groups=mesh['row'=16,'col'=8] {'row','col'}, dimensions={0} | all-to-all | bytes 1048576 | tf_op jit(solution)/shard_map/all_to_all | solution.py:17
  80.5 1.5 copy.37
  83.0 1.2 multiply_convert_fusion.5
  85.4 1.7 fusion.24
  87.1 2.4 %multiply_convert_fusion.4 = bf16[128,2048]{0,1:T(8,128)(2,1)} fusion(f32[2048,128]{1,0:T(8,128)S(1)} %get-tuple-element.36, f32[128,16,128]{0,2,1:T(8,128)S(1)} %copy.37, f32[2048]{0:T(1024)S(1)} %get-tuple-element.38, f32[2048]{0:T(1024)S(1)} %get-tuple-element.39, f32[128]{0:T(128)S(1)} %copy-done.22, f32[2048]{0:T(1024)S(1)} %rsqrt_bitcast_fusion, ...), kind=kLoop, calls=%fused_computation.62 | loop fusion | flops 2097152 | bytes 2654720 | tf_op jit(solution)/shard_map/convert_element_type | solution.py:96
  89.4 1.5 copy.38
  90.9 18.2 %all_to_all.32 = bf16[128,16,128]{2,1,0:T(8,128)(2,1)} all-to-all(bf16[128,16,128]{2,1,0:T(8,128)(2,1)S(1)} %copy.38), channel_id=1, replica_groups=mesh['row'=16,'col'=8] {'row','col'}, dimensions={0} | all-to-all | bytes 1048576 | tf_op jit(solution)/shard_map/all_to_all | solution.py:17
  109.1 1.6 reshape.192
  110.8 1.4 copy.39
  112.2 1.9 reshape.193
  114.2 2.3 %convolution_convert_fusion = bf16[512,512]{1,0:T(8,128)(2,1)} fusion(bf16[512,512]{1,0:T(8,128)(2,1)S(1)} %reshape.193, bf16[512,512]{1,0:T(8,128)(2,1)} %copy-done.14), kind=kOutput, calls=%fused_computation.10 | convolution fusion | flops 268697600 | bytes 1572864 | tf_op jit(solution)/shard_map/ij,ik->jk/dot_general | solution.py:60
  116.5 1.2 convolution_convert_fusion.1
  117.7 1.6 reshape.194
  119.3 1.2 copy.49
  120.5 2.4 %stack_reshape.14 = bf16[128,1,16,128]{3,2,0,1:T(8,128)(2,1)} reshape(bf16[16,8,32,64]{3,2,1,0:T(8,128)(2,1)} %bitcast.156) | data formatting | bytes 1048576 | tf_op jit(solution)/shard_map/stack;reshape | solution.py:100
  123.0 1.6 reshape.195
  124.6 1.2 copy.48
  125.8 1.8 stack_reshape.15
  128.8 1.2 copy.42
  129.9 6.0 %all-to-all-start.3 = ((bf16[128,2,16,128]{3,2,1,0:T(8,128)(2,1)}), bf16[128,2,16,128]{3,2,1,0:T(8,128)(2,1)}, u32[]{:S(2)}, u32[]{:S(2)}) async-start(bf16[128,2,16,128]{3,2,1,0:T(8,128)(2,1)} %copy.42), calls=%async_computation.3 | async-start | bytes 2097152 | tf_op jit(solution)/shard_map/all_to_all | solution.py:17
  136.2 2.2 %fusion.47 = f32[128,128]{1,0:T(8,128)} fusion(bf16[128,2048]{0,1:T(8,128)(2,1)} %copy-done.13, bf16[128,2048]{0,1:T(8,128)(2,1)} %copy-done.11), kind=kOutput, calls=%fused_computation.102 | convolution fusion | flops 67108864 | bytes 1114112 | tf_op jit(solution)/shard_map/hp,cp->hc/dot_general | solution.py:60
  138.4 2.2 %fusion.46 = f32[128,128]{1,0:T(8,128)} fusion(bf16[2048,128]{1,0:T(8,128)(2,1)} %bitcast.148, bf16[128,2048]{0,1:T(8,128)(2,1)} %get-tuple-element.18), kind=kOutput, calls=%fused_computation.101 | convolution fusion | flops 67108864 | bytes 1114112 | tf_op jit(solution)/shard_map/pc,dp->cd/dot_general | solution.py:60
  140.5 13.3 %all-to-all-done.3 = bf16[128,2,16,128]{3,2,1,0:T(8,128)(2,1)} async-done(((bf16[128,2,16,128]{3,2,1,0:T(8,128)(2,1)}), bf16[128,2,16,128]{3,2,1,0:T(8,128)(2,1)}, u32[]{:S(2)}, u32[]{:S(2)}) %all-to-all-start.3) | async-done | bytes 1048608 | tf_op jit(solution)/shard_map/all_to_all | solution.py:17
  153.8 2.7 %slice_convert_fusion.1 = (f32[128,1,16,128]{3,2,1,0:T(8,128)}, f32[128,1,16,128]{3,2,1,0:T(8,128)}) fusion(bf16[128,2,16,128]{3,2,1,0:T(8,128)(2,1)} %all-to-all-done.3), kind=kLoop, calls=%fused_computation.75 | loop fusion | flops 524288 | bytes 3145728 | tf_op jit(solution)/shard_map/convert_element_type | solution.py:101
  156.5 1.6 copy.43
  158.1 2.6 %copy.44 = f32[128,1,16,128]{0,3,2,1:T(8,128)} copy(f32[128,1,16,128]{3,2,1,0:T(8,128)} %get-tuple-element.21) | data formatting | bytes 2097152 | tf_op jit(solution)/shard_map/convert_element_type | solution.py:102
  160.6 2.4 %multiply_convert_fusion.3 = (bf16[128,2048]{0,1:T(8,128)(2,1)S(1)}, bf16[128,2048]{0,1:T(8,128)(2,1)S(1)}, bf16[128,2048]{0,1:T(8,128)(2,1)S(1)}, bf16[128,2048]{0,1:T(8,128)(2,1)S(1)}) fusion(f32[128,1,16,128]{0,3,2,1:T(8,128)S(1)} %copy.43, f32[2048]{0:T(1024)S(1)} %reshape.203, f32[256,2048]{0,1:T(8,128)} %copy-done.1, ...), kind=kLoop, calls=%fused_computation.61 | loop fusion | flops 5767168 | bytes 8396800 | tf_op jit(solution)/shard_map/convert.8
  164.2 1.4 fusion.36
  165.7 2.3 %fusion.42 = (f32[128]{0:T(128)}, f32[2048]{0:T(1024)S(1)}, f32[2048,128]{1,0:T(8,128)S(1)}) fusion(f32[128]{0:T(128)S(1)} %copy-done.21, f32[2048,128]{1,0:T(8,128)S(1)} %fusion.34, f32[2048,128]{1,0:T(8,128)} %fusion.36, bf16[128,2048]{0,1:T(8,128)(2,1)S(1)} %copy-done.12, bf16[128,128]{1,0:T(8,128)(2,1)S(1)} %copy-done.20), kind=kOutput, calls=%fused_computation.97 | convolution fusion | flops 68417408 | bytes 3712000 | tf_op jit(solution)/shard_map/dp,cd->pc/dot_general | solution.py:60
  169.2 18.5 %all_to_all.33 = f32[128,8,128]{2,1,0:T(8,128)S(1)} all-to-all(f32[128,8,128]{2,1,0:T(8,128)S(1)} %pad_bitcast_fusion), channel_id=1, replica_groups=mesh['row'=16,'col'=8] {'row','col'}, dimensions={0} | all-to-all | bytes 1048576 | tf_op jit(solution)/shard_map/all_to_all | solution.py:17
  188.7 4.9 %all-to-all-start.5 = ((f32[128,8,128]{2,1,0:T(8,128)}), f32[128,8,128]{2,1,0:T(8,128)S(1)}, u32[]{:S(2)}, u32[]{:S(2)}) async-start(f32[128,8,128]{2,1,0:T(8,128)} %broadcast_in_dim.2), calls=%async_computation.5 | async-start | bytes 1048576 | tf_op jit(solution)/shard_map/all_to_all | solution.py:17
  193.7 1.9 fusion.15
  195.6 11.4 %all-to-all-done.5 = f32[128,8,128]{2,1,0:T(8,128)S(1)} async-done(((f32[128,8,128]{2,1,0:T(8,128)}), f32[128,8,128]{2,1,0:T(8,128)S(1)}, u32[]{:S(2)}, u32[]{:S(2)}) %all-to-all-start.5) | async-done | bytes 524320 | tf_op jit(solution)/shard_map/all_to_all | solution.py:17
  (93 shorter events, 16.6 us)
Async XLA Ops:
  0.6 5.7 %copy-start = (bf16[128,256]{1,0:T(8,128)(2,1)S(1)}, bf16[128,256]{1,0:T(8,128)(2,1)}, u32[]{:S(2)}) copy-start(bf16[128,256]{1,0:T(8,128)(2,1)} %param.17) | copy-start | bytes 196612
  2.9 4.2 %copy-start.18 = (bf16[128,256]{1,0:T(8,128)(2,1)S(1)}, bf16[128,256]{1,0:T(8,128)(2,1)}, u32[]{:S(2)}) copy-start(bf16[128,256]{1,0:T(8,128)(2,1)} %param.16) | copy-start | bytes 196612
  6.3 0.8 copy-start.6
  7.6 1.3 copy-start.1
  47.3 7.2 %copy-start.9 = (bf16[512,512]{1,0:T(8,128)(2,1)}, bf16[512,512]{1,0:T(8,128)(2,1)S(1)}, u32[]{:S(2)}) copy-start(bf16[512,512]{1,0:T(8,128)(2,1)S(1)} %reshape.187) | copy-start | bytes 1572868
  54.5 0.8 copy-start.14
  61.2 20.8 %copy-start.22 = (f32[128]{0:T(128)S(1)}, f32[128]{0:T(128)}, u32[]{:S(2)}) copy-start(f32[128]{0:T(128)} %param.19) | copy-start | bytes 1540
  61.2 20.8 %copy-start.25 = (f32[128]{0:T(128)S(1)}, f32[128]{0:T(128)}, u32[]{:S(2)}) copy-start(f32[128]{0:T(128)} %param.20) | copy-start | bytes 1540
  79.7 0.8 copy-start.5
  79.7 2.9 %copy-start.19 = (bf16[128,128]{1,0:T(8,128)(2,1)S(1)}, bf16[128,128]{1,0:T(8,128)(2,1)}, u32[]{:S(2)}) copy-start(bf16[128,128]{1,0:T(8,128)(2,1)} %param.21) | copy-start | bytes 98308
  80.5 2.4 %copy-start.20 = (bf16[128,128]{1,0:T(8,128)(2,1)S(1)}, bf16[128,128]{1,0:T(8,128)(2,1)}, u32[]{:S(2)}) copy-start(bf16[128,128]{1,0:T(8,128)(2,1)} %param.18) | copy-start | bytes 98308
  82.0 1.0 copy-start.7
  82.6 1.6 copy-start.13
  83.0 1.2 copy-start.15
  85.4 4.1 %copy-start.11 = (bf16[128,2048]{0,1:T(8,128)(2,1)}, bf16[128,2048]{0,1:T(8,128)(2,1)S(1)}, u32[]{:S(2)}) copy-start(bf16[128,2048]{0,1:T(8,128)(2,1)S(1)} %get-tuple-element.19) | copy-start | bytes 1572868
  87.0 2.4 %copy-start.3 = (f32[2048,128]{1,0:T(8,128)}, f32[2048,128]{1,0:T(8,128)S(1)}, u32[]{:S(2)}) copy-start(f32[2048,128]{1,0:T(8,128)S(1)} %get-tuple-element.36) | copy-start | bytes 3145732
  112.2 4.3 %copy-start.10 = (bf16[512,512]{1,0:T(8,128)(2,1)S(1)}, bf16[512,512]{1,0:T(8,128)(2,1)}, u32[]{:S(2)}) copy-start(bf16[512,512]{1,0:T(8,128)(2,1)} %copy-done.9) | copy-start | bytes 1572868
  128.8 7.1 %copy-start.4 = (f32[2048,128]{1,0:T(8,128)S(1)}, f32[2048,128]{1,0:T(8,128)}, u32[]{:S(2)}) copy-start(f32[2048,128]{1,0:T(8,128)} %copy-done.3) | copy-start | bytes 3145732
  129.9 23.9 %all-to-all-start.3 = ((bf16[128,2,16,128]{3,2,1,0:T(8,128)(2,1)}), bf16[128,2,16,128]{3,2,1,0:T(8,128)(2,1)}, u32[]{:S(2)}, u32[]{:S(2)}) async-start(bf16[128,2,16,128]{3,2,1,0:T(8,128)(2,1)} %copy.42), calls=%async_computation.3 | async-start | bytes 2097152 | tf_op jit(solution)/shard_map/all_to_all | solution.py:17
  160.6 2.4 %copy-start.8 = (bf16[32,64,128]{2,1,0:T(8,128)(2,1)S(1)}, bf16[32,64,128]{2,1,0:T(8,128)(2,1)}, u32[]{:S(2)}) copy-start(bf16[32,64,128]{2,1,0:T(8,128)(2,1)} %copy-done.6) | copy-start | bytes 1572868
  163.9 1.8 copy-start.12
  163.9 1.8 copy-start.21
  165.6 2.4 %copy-start.2 = (bf16[32,64,128]{2,1,0:T(8,128)(2,1)S(1)}, bf16[32,64,128]{2,1,0:T(8,128)(2,1)}, u32[]{:S(2)}) copy-start(bf16[32,64,128]{2,1,0:T(8,128)(2,1)} %param.11) | copy-start | bytes 1572868
  168.0 1.1 copy-start.16
  168.0 1.1 copy-start.17
  168.0 1.1 copy-start.23
  168.0 1.1 copy-start.24
  188.7 18.3 %all-to-all-start.5 = ((f32[128,8,128]{2,1,0:T(8,128)}), f32[128,8,128]{2,1,0:T(8,128)S(1)}, u32[]{:S(2)}, u32[]{:S(2)}) async-start(f32[128,8,128]{2,1,0:T(8,128)} %broadcast_in_dim.2), calls=%async_computation.5 | async-start | bytes 1048576 | tf_op jit(solution)/shard_map/all_to_all | solution.py:17

commit v3 on v2

--- a/solution.py
+++ b/solution.py
@@ -1,6 +1,10 @@
+import functools
+
 import jax
 import jax.numpy as jnp
 from jax import lax
+from jax.experimental import pallas as pl
+from jax.experimental.pallas import tpu as pltpu
 from jax.sharding import PartitionSpec as P
 
 EPS = 1e-05
@@ -13,8 +17,54 @@
     return (center * inverse, inverse)
 
 
-def exchange(x):
-    return lax.all_to_all(x, AXES, 0, 0, tiled=True)
+MESH = pl.DeviceIdType.MESH
+
+
+def exchange_kernel(n_row, n_col, src, dst, send_sem, recv_sem):
+    n = n_row * n_col
+    me = lax.axis_index("row") * n_col + lax.axis_index("col")
+
+    def coords(p):
+        return (p // n_col, lax.rem(p, n_col))
+
+    def greet(d, carry):
+        peer = lax.rem(me + d, n)
+        pl.semaphore_signal(barrier, inc=1, device_id=coords(peer), device_id_type=MESH)
+        return carry
+
+    def send(d, carry):
+        peer = lax.rem(me + d, n)
+        pltpu.make_async_remote_copy(
+            src_ref=src.at[peer],
+            dst_ref=dst.at[me],
+            send_sem=send_sem,
+            recv_sem=recv_sem,
+            device_id=coords(peer),
+            device_id_type=MESH,
+        ).start()
+        return carry
+
+    barrier = pltpu.get_barrier_semaphore()
+    lax.fori_loop(1, n, greet, 0)
+    pl.semaphore_wait(barrier, n - 1)
+    lax.fori_loop(1, n, send, 0)
+    dst[me] = src[me]
+    others = dst.at[pl.ds(0, n - 1)]
+    pltpu.make_async_copy(others, others, recv_sem).wait()
+    pltpu.make_async_copy(others, others, send_sem).wait()
+
+
+def exchange(x, ident):
+    sizes = (lax.axis_size("row"), lax.axis_size("col"))
+    return pl.pallas_call(
+        functools.partial(exchange_kernel, *sizes),
+        out_shape=jax.ShapeDtypeStruct(x.shape, x.dtype),
+        in_specs=[pl.BlockSpec(memory_space=pltpu.VMEM)],
+        out_specs=pl.BlockSpec(memory_space=pltpu.VMEM),
+        scratch_shapes=[pltpu.SemaphoreType.DMA, pltpu.SemaphoreType.DMA],
+        compiler_params=pltpu.CompilerParams(collective_id=ident, has_side_effects=True),
+        name=f"exchange_{ident}",
+    )(x)
 
 
 def per_device(
@@ -43,7 +93,7 @@
     mask = (first_ok[:, None] & second_ok[None, :]).astype(jnp.float32).reshape(1, -1)
 
     def to_owner(tiles):
-        return exchange(jnp.stack([t.reshape(n, rows * cols // 128, 128) for t in tiles], axis=1))
+        return exchange(jnp.stack([t.reshape(n, rows * cols // 128, 128) for t in tiles], axis=1), 0)
 
     def whole(received):
         return received.reshape(n_row, n_col, rows, cols).transpose(0, 2, 1, 3).reshape(tokens, tokens)
@@ -71,7 +121,7 @@
     big_l = whole(got[:, 0])
     big_r = whole(got[:, 1])
     tri_own = dot("ik,jk->ij", big_l, big_r).astype(jnp.bfloat16)
-    tri = exchange(tiled(tri_own)).reshape(hidden, -1).astype(jnp.float32)
+    tri = exchange(tiled(tri_own), 1).reshape(hidden, -1).astype(jnp.float32)
     center = tri - jnp.mean(tri, axis=0, keepdims=True)
     tri_scale = lax.rsqrt(jnp.mean(center * center, axis=0, keepdims=True) + EPS)
     tri_hat = center * tri_scale
@@ -94,10 +144,10 @@
             - tri_hat * jnp.mean(hat_grad * tri_hat, axis=0, keepdims=True)
         )
     ).astype(jnp.bfloat16)
-    g = whole(exchange(tri_grad.reshape(n, rows * cols // 128, 128)))
+    g = whole(exchange(tri_grad.reshape(n, rows * cols // 128, 128), 2))
     row_own = dot("ij,jk->ik", g, big_r).astype(jnp.bfloat16)
     col_own = dot("ij,ik->jk", g, big_l).astype(jnp.bfloat16)
-    back = exchange(jnp.stack([tiled(row_own), tiled(col_own)], axis=1))
+    back = exchange(jnp.stack([tiled(row_own), tiled(col_own)], axis=1), 3)
     row_part = back[:, 0].reshape(hidden, -1).astype(jnp.float32)
     col_part = back[:, 1].reshape(hidden, -1).astype(jnp.float32)
 
@@ -133,8 +183,8 @@
     size = flat_parts.shape[0]
     per = -(-size // (n * 8)) * 8
     padded = jnp.pad(flat_parts, ((0, per * n - size), (0, 0))).reshape(n, per, 128)
-    mine = jnp.sum(exchange(padded), axis=0) * (1.0 / tokens)
-    total = exchange(jnp.broadcast_to(mine[None], (n,) + mine.shape)).reshape(n * per, 128)
+    mine = jnp.sum(exchange(padded, 4), axis=0) * (1.0 / tokens)
+    total = exchange(jnp.broadcast_to(mine[None], (n,) + mine.shape), 5).reshape(n * per, 128)
     done, at = [], 0
     for a in parts:
         count = a.size // 128

time: 211 us -> 227 us (1.076)
  Pallas kernels: 0 us -> 125 us
  blocking collectives: 84.7 us -> 0 us
  waiting for transfers between devices: 24.6 us -> 0 us
  starting transfers between devices: 10.9 us -> 0 us
  other arithmetic: 20.7 us -> 27.7 us
  local copies, waits for them, and re-layouts: 48.9 us -> 54.1 us
  matrix products: 18 us -> 14.8 us
    pallas_call x0 -> x6, Pallas kernels: none -> 125 us  [exchange(): pl.pallas_call(functools.partial(exchange_kernel, *sizes), out_shape=jax....]
    all_to_all x4 -> x0, blocking collectives: 84.7 us -> none  [exchange(): return lax.all_to_all(x, AXES, 0, 0, tiled=True)]
    all_to_all x2 -> x0, waiting for transfers between devices: 24.6 us -> none  [exchange(): return lax.all_to_all(x, AXES, 0, 0, tiled=True)]
    all_to_all x2 -> x0, starting transfers between devices: 10.9 us -> none  [exchange(): return lax.all_to_all(x, AXES, 0, 0, tiled=True)]
    transpose x3 -> x0, local copies, waits for them, and re-layouts: 5.51 us -> none  [whole(): received.reshape(n_row, n_col, rows, cols).transpose(0, 2, 1, 3)]
    another operation x2 -> x4, local copies, waits for them, and re-layouts: 4.23 us -> 8.3 us  [whole(): received.reshape(n_row, n_col, rows, cols).transpose(0, 2, 1, 3)]
    dot_general x15, matrix products: 18 us -> 14.8 us  [dot(): return jnp.einsum(form, a, b, preferred_element_type=jnp.float32)]
    slice x3, local copies, waits for them, and re-layouts: 1.25 us -> 3.76 us  [per_device(): done.append(total[at:at + count].reshape(a.shape))]
  transfers between devices with their start and end apart: 2 -> 0, of which waited for: 2 -> 0; matrix products, arithmetic and copies ran while one was open for 3% -> 0% of each run, Pallas kernels for 0% -> 0%
where the time goes in v3:
time: 227 us; the launch traced here: 224 us
  Pallas kernels  125 us (55%)
  local copies, waits for them, and re-layouts  54.1 us (24%)
  other arithmetic  27.7 us (12%)
  matrix products  14.8 us (7%)
    pallas_call x6, Pallas kernels, exchange(): pl.pallas_call(functools.partial(exchange_kernel, *sizes), out_shape=jax....  125 us
    dot_general x15, matrix products, dot(): return jnp.einsum(form, a, b, preferred_element_type=jnp.float32)  14.8 us
    reshape x5, local copies, waits for them, and re-layouts, whole(): received.reshape(n_row, n_col, rows, cols).transpose(0, 2, 1, 3)  8.8 us
    reshape x6, local copies, waits for them, and re-layouts, tiled(): t = matrix.reshape(n_row, rows, n_col, cols).transpose(0, 2, 1, 3)  8.54 us
    another operation x4, local copies, waits for them, and re-layouts, whole(): received.reshape(n_row, n_col, rows, cols).transpose(0, 2, 1, 3)  8.3 us

profile of v3, /device:TPU:0, one launch (start us, length us, event | category | flops | bytes accessed | tf_op | source)
XLA Modules:
  0.0 224.0 jit_solution(15718079380765353437)
XLA Ops:
  1.5 1.4 convert_reduce_fusion
  2.9 1.7 fusion.17
  4.7 1.7 fusion.11
  10.5 2.1 pad_maximum_fusion.src
  12.7 30.1 %exchange_0.1 = bf16[128,2,16,128]{3,2,1,0:T(8,128)(2,1)} custom-call(bf16[128,2,16,128]{3,2,1,0:T(8,128)(2,1)} %pad_maximum_fusion.src), custom_call_target="tpu_custom_call" | custom-call | tf_op jit(solution)/shard_map/exchange_0/pallas_call | solution.py:59
  42.8 2.4 %fusion.43 = (bf16[128,1,16,128]{3,2,1,0:T(8,128)(2,1)}, bf16[128,1,16,128]{3,2,1,0:T(8,128)(2,1)}) fusion(bf16[128,2,16,128]{3,2,1,0:T(8,128)(2,1)} %exchange_0.1), kind=kLoop, calls=%fused_computation.101 | loop fusion | bytes 2097152 | tf_op jit(solution)/shard_map/slice | solution.py:122
  45.1 1.6 reshape_squeeze.9
  46.8 1.4 copy.55
  48.2 1.9 reshape.187
  50.1 2.6 %reshape_squeeze.8 = bf16[16,8,32,64]{3,2,1,0:T(8,128)(2,1)} reshape(bf16[128,1,16,128]{3,2,1,0:T(8,128)(2,1)} %get-tuple-element.23) | data formatting | bytes 1048576 | tf_op jit(solution)/shard_map/reshape;squeeze | solution.py:99
  52.7 2.7 %copy.56 = bf16[16,8,32,64]{3,1,2,0:T(8,128)(2,1)} copy(bf16[16,8,32,64]{3,2,1,0:T(8,128)(2,1)} %reshape_squeeze.8) | data formatting | bytes 1048576 | tf_op jit(solution)/shard_map/reshape;squeeze | solution.py:99
  55.3 1.9 reshape.186
  58.0 1.3 convolution_convert_fusion.2
  59.3 1.6 reshape.188
  61.0 1.2 copy.54
  62.2 2.4 %reshape.189.src = bf16[128,16,128]{2,1,0:T(8,128)(2,1)} reshape(bf16[16,8,32,64]{3,2,1,0:T(8,128)(2,1)} %bitcast.160) | data formatting | bytes 1048576 | tf_op jit(solution)/shard_map/reshape | solution.py:103
  64.6 16.6 %exchange_1.1 = bf16[128,16,128]{2,1,0:T(8,128)(2,1)} custom-call(bf16[128,16,128]{2,1,0:T(8,128)(2,1)} %reshape.189.src), custom_call_target="tpu_custom_call" | custom-call | tf_op jit(solution)/shard_map/exchange_1/pallas_call | solution.py:59
  82.4 1.2 multiply_reduce_fusion.2
  83.7 1.5 copy.41
  86.2 1.2 multiply_convert_fusion.5
  88.5 2.6 %fusion.24 = (f32[128]{0:T(128)}, f32[2048]{0:T(1024)S(1)}, f32[2048]{0:T(1024)S(1)}, f32[2048,128]{1,0:T(8,128)}) fusion(f32[128,16,128]{0,2,1:T(8,128)S(1)} %copy.41, f32[2048]{0:T(1024)S(1)} %rsqrt_bitcast_fusion, f32[2048]{0:T(1024)S(1)} %get-tuple-element.30, f32[128]{0:T(128)S(1)} %copy-done.19, bf16[128,2048]{0,1:T(8,128)(2,1)S(1)} %get-tuple-element.19, ...), kind=kOutput, calls=%fused_computation.43 | convolution fusion | flops 69201792 | bytes 2688000 | tf_op jit(solution)/shard_map/cp,hc->hp/dot_general | solution.py:110
  91.1 1.5 reduce_sum.128
  92.6 3.8 %multiply_convert_fusion.4 = bf16[128,2048]{0,1:T(8,128)(2,1)} fusion(f32[2048,128]{1,0:T(8,128)} %get-tuple-element.36, f32[128,16,128]{0,2,1:T(8,128)S(1)} %copy.41, f32[2048]{0:T(1024)S(1)} %get-tuple-element.38, f32[2048]{0:T(1024)S(1)} %get-tuple-element.39, f32[128]{0:T(128)S(1)} %copy-done.19, f32[2048]{0:T(1024)S(1)} %rsqrt_bitcast_fusion, ...), kind=kLoop, calls=%fused_computation.65 | loop fusion | flops 2097152 | bytes 2654720 | tf_op jit(solution)/shard_map/convert_element_type | solution.py:146
  96.4 2.2 copy.42.src
  98.6 17.7 %exchange_2.1 = bf16[128,16,128]{2,1,0:T(8,128)(2,1)} custom-call(bf16[128,16,128]{2,1,0:T(8,128)(2,1)} %copy.42.src), custom_call_target="tpu_custom_call" | custom-call | tf_op jit(solution)/shard_map/exchange_2/pallas_call | solution.py:59
  116.4 1.6 reshape.192
  118.0 1.4 copy.53
  119.5 1.9 reshape.193
  121.4 2.3 %convolution_convert_fusion = bf16[512,512]{1,0:T(8,128)(2,1)} fusion(bf16[512,512]{1,0:T(8,128)(2,1)S(1)} %reshape.193, bf16[512,512]{1,0:T(8,128)(2,1)} %copy-done.10), kind=kOutput, calls=%fused_computation.10 | convolution fusion | flops 268697600 | bytes 1572864 | tf_op jit(solution)/shard_map/ij,ik->jk/dot_general | solution.py:110
  123.7 1.2 convolution_convert_fusion.1
  125.0 1.6 reshape.194
  126.6 1.2 copy.52
  127.8 2.4 %stack_reshape.14 = bf16[128,1,16,128]{3,2,1,0:T(8,128)(2,1)} reshape(bf16[16,8,32,64]{3,2,1,0:T(8,128)(2,1)} %bitcast.162) | data formatting | bytes 1048576 | tf_op jit(solution)/shard_map/stack;reshape | solution.py:150
  130.3 1.6 reshape.195
  131.9 1.2 copy.51
  133.1 1.8 stack_reshape.15
  134.9 2.1 pad_maximum_fusion.1.src
  137.0 27.1 %exchange_3.1 = bf16[128,2,16,128]{3,2,1,0:T(8,128)(2,1)} custom-call(bf16[128,2,16,128]{3,2,1,0:T(8,128)(2,1)} %pad_maximum_fusion.1.src), custom_call_target="tpu_custom_call" | custom-call | tf_op jit(solution)/shard_map/exchange_3/pallas_call | solution.py:59
  164.1 2.7 %slice_convert_fusion.1 = (f32[128,1,16,128]{3,2,1,0:T(8,128)}, f32[128,1,16,128]{3,2,1,0:T(8,128)}) fusion(bf16[128,2,16,128]{3,2,1,0:T(8,128)(2,1)} %exchange_3.1), kind=kLoop, calls=%fused_computation.80 | loop fusion | flops 524288 | bytes 3145728 | tf_op jit(solution)/shard_map/convert_element_type | solution.py:151
  166.8 1.6 copy.43
  168.4 2.6 %copy.44 = f32[128,1,16,128]{0,3,2,1:T(8,128)} copy(f32[128,1,16,128]{3,2,1,0:T(8,128)} %get-tuple-element.21) | data formatting | bytes 2097152 | tf_op jit(solution)/shard_map/convert_element_type | solution.py:152
  171.0 2.4 %multiply_convert_fusion.3 = (bf16[128,2048]{0,1:T(8,128)(2,1)S(1)}, bf16[128,2048]{0,1:T(8,128)(2,1)S(1)}, bf16[128,2048]{0,1:T(8,128)(2,1)S(1)}, bf16[128,2048]{0,1:T(8,128)(2,1)S(1)}) fusion(f32[128,1,16,128]{0,3,2,1:T(8,128)S(1)} %copy.43, f32[2048]{0:T(1024)S(1)} %reshape.203, f32[256,2048]{0,1:T(8,128)} %copy-done.1, ...), kind=kLoop, calls=%fused_computation.64 | loop fusion | flops 5767168 | bytes 8396800 | tf_op jit(solution)/shard_map/convert.8
  175.3 1.6 fusion.36
  180.1 2.0 fusion.15
  182.9 15.8 %exchange_4.1 = f32[128,8,128]{2,1,0:T(8,128)} custom-call(f32[128,8,128]{2,1,0:T(8,128)} %pad_bitcast_fusion.src), custom_call_target="tpu_custom_call" | custom-call | tf_op jit(solution)/shard_map/exchange_4/pallas_call | solution.py:59
  200.7 18.1 %exchange_5.1 = f32[128,8,128]{2,1,0:T(8,128)} custom-call(f32[128,8,128]{2,1,0:T(8,128)} %broadcast_in_dim.2.src), custom_call_target="tpu_custom_call" | custom-call | tf_op jit(solution)/shard_map/exchange_5/pallas_call | solution.py:59
  218.8 1.2 slice.66
  220.1 1.5 slice_bitcast_fusion
  (84 shorter events, 18.5 us)
Async XLA Ops:
  0.6 5.7 %copy-start = (bf16[128,256]{1,0:T(8,128)(2,1)S(1)}, bf16[128,256]{1,0:T(8,128)(2,1)}, u32[]{:S(2)}) copy-start(bf16[128,256]{1,0:T(8,128)(2,1)} %param.17) | copy-start | bytes 196612
  2.9 4.2 %copy-start.14 = (bf16[128,256]{1,0:T(8,128)(2,1)S(1)}, bf16[128,256]{1,0:T(8,128)(2,1)}, u32[]{:S(2)}) copy-start(bf16[128,256]{1,0:T(8,128)(2,1)} %param.16) | copy-start | bytes 196612
  6.3 0.8 copy-start.3
  7.6 1.4 copy-start.1
  50.1 7.1 %copy-start.6 = (bf16[512,512]{1,0:T(8,128)(2,1)}, bf16[512,512]{1,0:T(8,128)(2,1)S(1)}, u32[]{:S(2)}) copy-start(bf16[512,512]{1,0:T(8,128)(2,1)S(1)} %reshape.187) | copy-start | bytes 1572868
  57.2 0.8 copy-start.10
  64.6 20.5 %copy-start.19 = (f32[128]{0:T(128)S(1)}, f32[128]{0:T(128)}, u32[]{:S(2)}) copy-start(f32[128]{0:T(128)} %param.19) | copy-start | bytes 1540
  64.6 20.6 %copy-start.22 = (f32[128]{0:T(128)S(1)}, f32[128]{0:T(128)}, u32[]{:S(2)}) copy-start(f32[128]{0:T(128)} %param.20) | copy-start | bytes 1540
  81.2 4.6 %copy-start.16 = (bf16[128,128]{1,0:T(8,128)(2,1)S(1)}, bf16[128,128]{1,0:T(8,128)(2,1)}, u32[]{:S(2)}) copy-start(bf16[128,128]{1,0:T(8,128)(2,1)} %param.21) | copy-start | bytes 98308
  83.7 2.4 %copy-start.17 = (bf16[128,128]{1,0:T(8,128)(2,1)S(1)}, bf16[128,128]{1,0:T(8,128)(2,1)}, u32[]{:S(2)}) copy-start(bf16[128,128]{1,0:T(8,128)(2,1)} %param.18) | copy-start | bytes 98308
  85.2 1.0 copy-start.4
  86.2 1.2 copy-start.13
  87.8 3.3 %copy-start.8 = (bf16[128,2048]{0,1:T(8,128)(2,1)}, bf16[128,2048]{0,1:T(8,128)(2,1)S(1)}, u32[]{:S(2)}) copy-start(bf16[128,2048]{0,1:T(8,128)(2,1)S(1)} %get-tuple-element.18) | copy-start | bytes 1572868
  119.5 4.3 %copy-start.7 = (bf16[512,512]{1,0:T(8,128)(2,1)S(1)}, bf16[512,512]{1,0:T(8,128)(2,1)}, u32[]{:S(2)}) copy-start(bf16[512,512]{1,0:T(8,128)(2,1)} %copy-done.6) | copy-start | bytes 1572868
  171.0 2.4 %copy-start.5 = (bf16[32,64,128]{2,1,0:T(8,128)(2,1)S(1)}, bf16[32,64,128]{2,1,0:T(8,128)(2,1)}, u32[]{:S(2)}) copy-start(bf16[32,64,128]{2,1,0:T(8,128)(2,1)} %copy-done.3) | copy-start | bytes 1572868
  173.4 1.4 copy-start.11
  173.4 1.4 copy-start.12
  174.5 0.8 copy-start.15
  174.8 2.1 copy-start.9
  174.8 2.1 copy-start.18
  177.0 2.0 copy-start.2
  177.9 2.1 copy-start.20
  177.9 2.1 copy-start.21

commit v4 on v2

v4 whole, which is shorter than its diff:
```python
import functools

import jax
import jax.numpy as jnp
from jax import lax
from jax.experimental import pallas as pl
from jax.experimental.pallas import tpu as pltpu
from jax.sharding import PartitionSpec as P

EPS = 1e-05
MESH = pl.DeviceIdType.MESH
BF = jnp.bfloat16
F32 = jnp.float32
LANES = 128
GROUP = 4


def dot(a, b):
    return jnp.dot(a, b, preferred_element_type=F32)


def dot_last(a, b):
    return lax.dot_general(a, b, (((1,), (1,)), ((), ())), preferred_element_type=F32)


def dot_first(a, b):
    return lax.dot_general(a, b, (((0,), (0,)), ((), ())), preferred_element_type=F32)


def center_scale(values):
    center = values - jnp.mean(values, axis=0, keepdims=True)
    inverse = lax.rsqrt(jnp.mean(center * center, axis=0, keepdims=True) + EPS)
    return center * inverse, inverse


def norm_back(grad, hat, scale):
    mean = jnp.mean(grad, axis=0, keepdims=True)
    along = jnp.mean(grad * hat, axis=0, keepdims=True)
    return scale * (grad - mean - hat * along)


def halves(a, b):
    half = a.shape[1] // 2
    first = lax.broadcasted_iota(jnp.int32, a.shape, 1) < half
    return (
        jnp.where(first, a, pltpu.roll(b, half, 1)),
        jnp.where(first, pltpu.roll(a, half, 1), b),
    )


def column(row_ref):
    return jnp.transpose(jnp.broadcast_to(row_ref[...], (LANES, LANES)))[:, :1]


def kernel(
    n_row,
    n_col,
    pair,
    cotangent,
    length,
    norm_gain,
    norm_bias,
    left_weight,
    right_weight,
    gate_weight,
    out_gain,
    out_bias,
    out_weight,
    update,
    grad_pair,
    grad_left,
    grad_right,
    grad_gating,
    grad_output,
    grad_norms,
    stage,
    hat_s,
    scale_s,
    normed_s,
    coef_s,
    gate_s,
    tnormed_s,
    ograd_s,
    ggrad_s,
    back_s,
    comb_s,
    big_l,
    big_r,
    big_g,
    send_a,
    recv_a,
    send_b,
    recv_b,
    send_c,
    recv_c,
    send_d,
    recv_d,
    send_e,
    recv_e,
    send_f,
    recv_f,
    send_sem,
    recv_sem,
):
    n = n_row * n_col
    rows, cols, chan = pair.shape
    hidden = out_weight.shape[0]
    blocks = rows * cols // LANES
    apart = LANES // cols * 8
    del apart
    tokens = n_row * rows
    half = rows // 2
    wide = GROUP * LANES
    row = lax.axis_index("row")
    col = lax.axis_index("col")
    me = row * n_col + col

    def coords(p):
        return (p // n_col, lax.rem(p, n_col))

    barrier = pltpu.get_barrier_semaphore()

    def greet(d, carry):
        peer = lax.rem(me + d, n)
        pl.semaphore_signal(barrier, inc=1, device_id=coords(peer), device_id_type=MESH)
        return carry

    def start_all(phase, src, dst, same=False):
        def send(d, carry):
            peer = lax.rem(me + d, n)
            pltpu.make_async_remote_copy(
                src_ref=src if same else src.at[peer],
                dst_ref=dst.at[me],
                send_sem=send_sem.at[phase],
                recv_sem=recv_sem.at[phase],
                device_id=coords(peer),
                device_id_type=MESH,
            ).start()
            return carry

        lax.fori_loop(1, n, send, 0)
        dst[me] = src[...] if same else src[me]

    def wait_on(sems, phase, dst):
        others = dst.at[pl.ds(0, n - 1)]
        pltpu.make_async_copy(others, others, sems.at[phase]).wait()

    def pack(dst, count, stride):
        def body(h, carry):
            at = pl.multiple_of(h * stride, 8)
            dst[h] = stage[pl.ds(at, count), :].astype(BF)
            return carry

        lax.fori_loop(0, n, body, 0, unroll=8)

    def unpack(src, count, stride):
        def body(h, carry):
            at = pl.multiple_of(h * stride, 8)
            stage[pl.ds(at, count), :] = src[h].astype(F32)
            return carry

        lax.fori_loop(0, n, body, 0, unroll=8)

    def spread(values, first, stride):
        for t in range(values.shape[1] // LANES):
            stage[pl.ds(first + t, LANES, stride=stride), :] = values[:, t * LANES : (t + 1) * LANES]

    def collect(first, stride, count):
        return jnp.concatenate(
            [stage[pl.ds(first + t, LANES, stride=stride), :] for t in range(count)], axis=1
        )

    def channels_first(ref, first):
        parts = []
        for t in range(GROUP):
            block = jnp.concatenate([ref[first + t], ref[first + t + half]], axis=0)
            parts.append(jnp.transpose(block.astype(F32)))
        return jnp.concatenate(parts, axis=1)

    def positions_first(ref, first, values):
        for t in range(GROUP):
            block = jnp.transpose(values[:, t * LANES : (t + 1) * LANES]).astype(BF)
            ref[first + t] = block[:cols]
            ref[first + t + half] = block[cols:]

    def lanes_at(first):
        return pl.ds(pl.multiple_of(first * LANES, LANES), wide)

    def assemble(src, at, dst):
        def body(r, carry):
            for q in range(n_col // 2):
                a = src[r * n_col + 2 * q, at : at + half, :].astype(F32)
                b = src[r * n_col + 2 * q + 1, at : at + half, :].astype(F32)
                low, high = halves(a, b)
                base = pl.multiple_of(r * rows, rows)
                dst[pl.ds(base, half), q * LANES : (q + 1) * LANES] = low.astype(BF)
                dst[pl.ds(base + half, half), q * LANES : (q + 1) * LANES] = high.astype(BF)
            return carry

        lax.fori_loop(0, n_row, body, 0, unroll=2)

    def disassemble(values, dst, at):
        for r in range(n_row):
            for q in range(n_col // 2):
                low = values[r * rows : r * rows + half, q * LANES : (q + 1) * LANES]
                high = values[r * rows + half : (r + 1) * rows, q * LANES : (q + 1) * LANES]
                a, b = halves(low, high)
                dst[r * n_col + 2 * q, at : at + half, :] = a.astype(BF)
                dst[r * n_col + 2 * q + 1, at : at + half, :] = b.astype(BF)

    lax.fori_loop(1, n, greet, 0)

    gain = column(norm_gain)
    bias = column(norm_bias)
    forward_weight = jnp.concatenate(
        [
            jnp.transpose(left_weight[...]),
            jnp.transpose(right_weight[...]),
            jnp.transpose(gate_weight[...]),
        ],
        axis=0,
    )

    def first_pass(g, carry):
        first = g * GROUP
        at = lanes_at(first)
        hat, scale = center_scale(channels_first(pair, first))
        normed = (hat * gain + bias).astype(BF)
        hat_s[:, at] = hat
        scale_s[:, at] = scale
        normed_s[:, at] = normed
        lane = lax.broadcasted_iota(jnp.int32, (1, wide), 1)
        inner = lax.rem(lane, LANES)
        i = row * rows + first + lane // LANES + inner // cols * half
        k = col * cols + lax.rem(inner, cols)
        real = length[0]
        mask = jnp.where((i < real) & (k < real), 1.0, 0.0).astype(F32)
        proj = dot(forward_weight, normed)
        for side in range(2):
            base = 2 * hidden * side
            sig = mask * jax.nn.sigmoid(proj[base + hidden : base + 2 * hidden])
            act = sig * proj[base : base + hidden]
            coef_s[2 * side, :, at] = sig
            coef_s[2 * side + 1, :, at] = act * (1.0 - sig)
            spread(act, first + side * blocks, 40)
        gate_s[:, at] = jax.nn.sigmoid(proj[4 * hidden :])
        return carry

    lax.fori_loop(0, blocks // GROUP, first_pass, 0)
    pack(send_a, 2 * blocks, 40)
    pl.semaphore_wait(barrier, n - 1)
    start_all(0, send_a, recv_a)

    wait_on(recv_sem, 0, recv_a)
    assemble(recv_a, 0, big_l)
    assemble(recv_a, blocks, big_r)
    disassemble(dot_last(big_l[...], big_r[...]), send_b, 0)
    start_all(1, send_b, recv_b)

    o_gain = column(out_gain)
    o_bias = column(out_bias)
    out_back = out_weight[...]
    out_forward = jnp.transpose(out_back)
    wait_on(recv_sem, 1, recv_b)
    unpack(recv_b, blocks, 24)

    def second_pass(g, carry):
        first = g * GROUP
        at = lanes_at(first)
        hat, scale = center_scale(collect(first, 24, GROUP))
        tri_normed = (hat * o_gain + o_bias).astype(BF)
        tnormed_s[:, at] = tri_normed
        outer = dot(out_forward, tri_normed)
        gate = gate_s[:, at]
        gated = gate * outer
        positions_first(update, first, gated)
        upstream = channels_first(cotangent, first)
        outer_grad = (upstream * gate).astype(BF)
        ograd_s[:, at] = outer_grad
        ggrad_s[:, at] = (upstream * gated * (1.0 - gate)).astype(BF)
        tnorm_grad = dot(out_back, outer_grad)
        spread(norm_back(tnorm_grad * o_gain, hat, scale), first, 24)
        along = tnorm_grad * hat
        return (
            carry[0] + jnp.sum(along, axis=1, keepdims=True),
            carry[1] + jnp.sum(tnorm_grad, axis=1, keepdims=True),
        )

    zero = jnp.zeros((hidden, 1), F32)
    o_gain_grad, o_bias_grad = lax.fori_loop(0, blocks // GROUP, second_pass, (zero, zero))
    pack(send_c, blocks, 24)
    start_all(2, send_c, recv_c)
    back_s[...] = dot(gate_weight[...], ggrad_s[...])
    part_output = dot_last(tnormed_s[...], ograd_s[...])
    part_gating = dot_last(normed_s[...], ggrad_s[...])

    wait_on(recv_sem, 2, recv_c)
    assemble(recv_c, 0, big_g)
    disassemble(dot(big_g[...], big_r[...]), send_d, 0)
    disassemble(dot_first(big_g[...], big_l[...]), send_d, blocks)
    start_all(3, send_d, recv_d)

    backward_weight = jnp.concatenate([left_weight[...], right_weight[...]], axis=1)
    wait_on(recv_sem, 3, recv_d)
    unpack(recv_d, 2 * blocks, 40)

    def third_pass(g, carry):
        first = g * GROUP
        at = lanes_at(first)
        from_row = collect(first, 40, GROUP)
        from_col = collect(first + blocks, 40, GROUP)
        comb = jnp.concatenate(
            [
                from_row * coef_s[0, :, at],
                from_row * coef_s[1, :, at],
                from_col * coef_s[2, :, at],
                from_col * coef_s[3, :, at],
            ],
            axis=0,
        ).astype(BF)
        comb_s[:, at] = comb
        normed_grad = back_s[:, at] + dot(backward_weight, comb)
        back_s[:, at] = normed_grad
        along = normed_grad * hat_s[:, at]
        return (
            carry[0] + jnp.sum(along, axis=1, keepdims=True),
            carry[1] + jnp.sum(normed_grad, axis=1, keepdims=True),
        )

    gain_grad, bias_grad = lax.fori_loop(0, blocks // GROUP, third_pass, (zero, zero))
    spread(dot_last(normed_s[...], comb_s[...]), 0, 24)
    spread(part_gating, 4, 24)
    spread(part_output, 5, 24)
    lane = lax.broadcasted_iota(jnp.int32, (LANES, LANES), 1)
    norms = jnp.where(lane == 0, gain_grad, 0.0)
    norms = jnp.where(lane == 1, bias_grad, norms)
    norms = jnp.where(lane == 2, o_gain_grad, norms)
    norms = jnp.where(lane == 3, o_bias_grad, norms)
    spread(norms, 6, 24)
    spread(jnp.zeros_like(norms), 7, 24)
    pack(send_e, 8, 24)
    start_all(4, send_e, recv_e)

    def fourth_pass(g, carry):
        first = g * GROUP
        at = lanes_at(first)
        grad = norm_back(back_s[:, at] * gain, hat_s[:, at], scale_s[:, at])
        positions_first(grad_pair, first, grad)
        return carry

    lax.fori_loop(0, blocks // GROUP, fourth_pass, 0)

    wait_on(recv_sem, 4, recv_e)

    def add(p, total):
        return total + recv_e[p].astype(F32)

    total = lax.fori_loop(0, n, add, jnp.zeros((8, LANES), F32), unroll=8)
    send_f[...] = (total * (1.0 / tokens)).astype(BF)
    start_all(5, send_f, recv_f, same=True)
    wait_on(recv_sem, 5, recv_f)
    unpack(recv_f, 8, 24)
    grad_left[...] = collect(0, 24, 2)
    grad_right[...] = collect(2, 24, 2)
    grad_gating[...] = collect(4, 24, 1)
    grad_output[...] = collect(5, 24, 1)
    grad_norms[...] = jnp.transpose(collect(6, 24, 1))[:4]
    for phase, dst in enumerate((recv_a, recv_b, recv_c, recv_d, recv_e, recv_f)):
        wait_on(send_sem, phase, dst)


def per_device(pair, cotangent, length, *weights):
    n_row = lax.axis_size("row")
    n_col = lax.axis_size("col")
    n = n_row * n_col
    rows, cols, chan = pair.shape
    hidden = weights[-1].shape[0]
    tokens = n_row * rows
    places = rows * cols
    blocks = places // LANES
    weights = [w.reshape(1, -1) if w.ndim == 1 else w for w in weights]
    vmem = pl.BlockSpec(memory_space=pltpu.VMEM)
    smem = pl.BlockSpec(memory_space=pltpu.SMEM)
    shape = jax.ShapeDtypeStruct
    return pl.pallas_call(
        functools.partial(kernel, n_row, n_col),
        out_shape=(
            shape(pair.shape, BF),
            shape(pair.shape, BF),
            shape((chan, 2 * hidden), F32),
            shape((chan, 2 * hidden), F32),
            shape((chan, chan), F32),
            shape((hidden, chan), F32),
            shape((4, chan), F32),
        ),
        in_specs=[vmem, vmem, smem] + [vmem] * len(weights),
        out_specs=(vmem,) * 7,
        scratch_shapes=[
            pltpu.VMEM((n * 40, LANES), F32),
            pltpu.VMEM((chan, places), F32),
            pltpu.VMEM((1, places), F32),
            pltpu.VMEM((chan, places), BF),
            pltpu.VMEM((4, hidden, places), F32),
            pltpu.VMEM((chan, places), F32),
            pltpu.VMEM((hidden, places), BF),
            pltpu.VMEM((chan, places), BF),
            pltpu.VMEM((chan, places), BF),
            pltpu.VMEM((chan, places), F32),
            pltpu.VMEM((4 * hidden, places), BF),
            pltpu.VMEM((tokens, tokens), BF),
            pltpu.VMEM((tokens, tokens), BF),
            pltpu.VMEM((tokens, tokens), BF),
            pltpu.VMEM((n, 2 * blocks, LANES), BF),
            pltpu.VMEM((n, 2 * blocks, LANES), BF),
            pltpu.VMEM((n, blocks, LANES), BF),
            pltpu.VMEM((n, blocks, LANES), BF),
            pltpu.VMEM((n, blocks, LANES), BF),
            pltpu.VMEM((n, blocks, LANES), BF),
            pltpu.VMEM((n, 2 * blocks, LANES), BF),
            pltpu.VMEM((n, 2 * blocks, LANES), BF),
            pltpu.VMEM((n, 8, LANES), BF),
            pltpu.VMEM((n, 8, LANES), BF),
            pltpu.VMEM((8, LANES), BF),
            pltpu.VMEM((n, 8, LANES), BF),
            pltpu.SemaphoreType.DMA((6,)),
            pltpu.SemaphoreType.DMA((6,)),
        ],
        compiler_params=pltpu.CompilerParams(
            collective_id=0, has_side_effects=True, vmem_limit_bytes=56 << 20
        ),
        name="triangle",
    )(pair, cotangent, length, *weights)


def solution(mesh):
    return jax.shard_map(
        per_device,
        mesh=mesh,
        in_specs=(P("row", "col", None), P("row", "col", None)) + (P(),) * 9,
        out_specs=(P("row", "col", None), P("row", "col", None)) + (P(),) * 5,
        check_vma=False,
    )
```

time: 211 us -> 102 us (0.48)
  Pallas kernels: 0 us -> 92.3 us
  blocking collectives: 84.7 us -> 0 us
  local copies, waits for them, and re-layouts: 48.9 us -> 6.88 us
  waiting for transfers between devices: 24.6 us -> 0 us
  other arithmetic: 20.7 us -> 0 us
  matrix products: 18 us -> 0 us
  starting transfers between devices: 10.9 us -> 0 us
    pallas_call x0 -> x1, Pallas kernels: none -> 92.3 us  [per_device(): pl.pallas_call(functools.partial(kernel, n_row, n_col), out_shape=(shape(...]
    all_to_all x4 -> x0, blocking collectives: 84.7 us -> none  [exchange(): return lax.all_to_all(x, AXES, 0, 0, tiled=True)]
    all_to_all x2 -> x0, waiting for transfers between devices: 24.6 us -> none  [exchange(): return lax.all_to_all(x, AXES, 0, 0, tiled=True)]
    reshape x17 -> x0, local copies, waits for them, and re-layouts: 20.6 us -> none  [the longest x6 8.55 us: tiled(): t = matrix.reshape(n_row, rows, n_col, cols).transpose(0, 2, 1, 3)]
    dot_general x15 -> x0, matrix products: 18 us -> none  [dot(): return jnp.einsum(form, a, b, preferred_element_type=jnp.float32)]
    another operation x7 -> x0, local copies, waits for them, and re-layouts: 11.2 us -> none  [the longest x3 5.38 us: per_device(): back = exchange(jnp.stack([tiled(row_own), tiled(col_own)], axis=1))]
    convert_element_type x8 -> x0, other arithmetic: 11.1 us -> none  [the longest x1 2.7 us: per_device(): row_part = back[:, 0].reshape(hidden, -1).astype(jnp.float32)]
    all_to_all x2 -> x0, starting transfers between devices: 10.9 us -> none  [exchange(): return lax.all_to_all(x, AXES, 0, 0, tiled=True)]
  transfers between devices with their start and end apart: 2 -> 0, of which waited for: 2 -> 0; matrix products, arithmetic and copies ran while one was open for 3% -> 0% of each run, Pallas kernels for 0% -> 0%
where the time goes in v4:
time: 102 us; the launch traced here: 101 us
  Pallas kernels  92.3 us (90%)
  local copies, waits for them, and re-layouts  6.88 us (7%)
  between operations  1.31 us (1%)
    pallas_call x1, Pallas kernels, per_device(): pl.pallas_call(functools.partial(kernel, n_row, n_col), out_shape=(shape(...  92.3 us
    unnamed x19, local copies, waits for them, and re-layouts  6.88 us

profile of v4, /device:TPU:0, one launch (start us, length us, event | category | flops | bytes accessed | tf_op | source)
XLA Modules:
  0.0 100.5 jit_solution(569156137778542095)
XLA Ops:
  1.3 92.3 %triangle.1 = (bf16[32,64,128]{2,1,0:T(8,128)(2,1)}, bf16[32,64,128]{2,1,0:T(8,128)(2,1)}, f32[128,256]{1,0:T(8,128)}, f32[128,256]{1,0:T(8,128)}, f32[128,128]{...) custom-call(bf16[32,64,128]{2,1,0:T(8,128)(2,1)} %pair.1, bf16[32,64,128]{2,1,0:T(8,128)(2,1)} %cotangent.1, ...), custom_call_target="tpu_custom_call" | custom-call | tf_op jit(solution)/shard_map/triangle/pallas_call | solution.py:385
  93.6 0.0 copy-start
  93.6 1.9 %copy.26 = bf16[32,64,128]{2,1,0:T(8,128)(2,1)} copy(bf16[32,64,128]{2,1,0:T(8,128)(2,1)} %get-tuple-element.14) | data formatting | bytes 1048576
  95.6 0.0 copy-done
  95.6 0.0 copy-start.2
  95.6 0.8 copy.27
  96.4 0.2 copy-done.2
  96.6 0.0 copy-start.1
  96.6 0.7 copy.28
  97.3 0.3 copy-done.1
  97.5 0.0 copy-start.4
  97.6 0.7 copy.29
  98.2 0.2 copy-done.4
  98.4 0.0 copy-start.3
  98.4 0.6 copy.30
  99.0 0.2 copy-done.3
  99.3 0.0 copy-start.5
  99.3 0.6 copy.31
  99.9 0.1 copy-done.5
  100.0 0.6 copy.32
Async XLA Ops:
  93.6 1.9 %copy-start = (bf16[32,64,128]{2,1,0:T(8,128)(2,1)S(1)}, bf16[32,64,128]{2,1,0:T(8,128)(2,1)}, u32[]{:S(2)}) copy-start(bf16[32,64,128]{2,1,0:T(8,128)(2,1)} %get-tuple-element.15) | copy-start | bytes 1572868
  95.6 1.0 %copy-start.2 = (f32[128,256]{1,0:T(8,128)S(1)}, f32[128,256]{1,0:T(8,128)}, u32[]{:S(2)}) copy-start(f32[128,256]{1,0:T(8,128)} %get-tuple-element.16) | copy-start | bytes 393220
  96.6 1.0 copy-start.1
  97.5 0.9 copy-start.4
  98.4 0.9 copy-start.3
  99.3 0.7 copy-start.5

commit v5 on v4

--- a/solution.py
+++ b/solution.py
@@ -52,27 +52,72 @@
     return jnp.transpose(jnp.broadcast_to(row_ref[...], (LANES, LANES)))[:, :1]
 
 
+def distance(step):
+    return sum(min(d, 4 - d) for d in step[:3])
+
+
+STEPS = [
+    (dx, dy, dz, dc)
+    for dx in range(4)
+    for dy in range(4)
+    for dz in range(4)
+    for dc in range(2)
+    if (dx, dy, dz, dc) != (0, 0, 0, 0)
+]
+STEPS.sort(key=lambda step: (-distance(step), step[3]))
+
+
+def peers(row, col):
+    z = row // 8 * 2 + lax.rem(col, 2)
+    x = lax.rem(row // 2, 4)
+    core = lax.rem(row, 2)
+    y = col // 2
+    at_x = [lax.rem(x + d, 4) * 2 for d in range(4)]
+    at_y = [lax.rem(y + d, 4) * 2 for d in range(4)]
+    at_z = [lax.rem(z + d, 4) for d in range(4)]
+    high = [q // 2 * 8 for q in at_z]
+    low = [lax.rem(q, 2) for q in at_z]
+    at_core = [core, 1 - core]
+    found = []
+    for dx, dy, dz, dc in STEPS:
+        to_row = high[dz] + at_x[dx] + at_core[dc]
+        to_col = at_y[dy] + low[dz]
+        found.append((to_row, to_col, to_row * 8 + to_col))
+    return found
+
+
 def kernel(
     n_row,
     n_col,
+    pair_hbm,
+    cotangent_hbm,
+    length,
+    *refs,
+):
+    weights_hbm, refs = refs[:8], refs[8:]
+    kernel_body(n_row, n_col, pair_hbm, cotangent_hbm, length, weights_hbm, *refs)
+
+
+def kernel_body(
+    n_row,
+    n_col,
+    pair_hbm,
+    cotangent_hbm,
+    length,
+    weights_hbm,
+    update,
+    grad_pair,
+    recv_f,
     pair,
-    cotangent,
-    length,
     norm_gain,
     norm_bias,
     left_weight,
     right_weight,
     gate_weight,
+    cotangent,
     out_gain,
     out_bias,
     out_weight,
-    update,
-    grad_pair,
-    grad_left,
-    grad_right,
-    grad_gating,
-    grad_output,
-    grad_norms,
     stage,
     hat_s,
     scale_s,
@@ -98,16 +143,14 @@
     send_e,
     recv_e,
     send_f,
-    recv_f,
     send_sem,
     recv_sem,
+    load_sem,
 ):
     n = n_row * n_col
     rows, cols, chan = pair.shape
     hidden = out_weight.shape[0]
     blocks = rows * cols // LANES
-    apart = LANES // cols * 8
-    del apart
     tokens = n_row * rows
     half = rows // 2
     wide = GROUP * LANES
@@ -115,35 +158,35 @@
     col = lax.axis_index("col")
     me = row * n_col + col
 
-    def coords(p):
-        return (p // n_col, lax.rem(p, n_col))
-
+    early = (pair, norm_gain, norm_bias, left_weight, right_weight, gate_weight)
+    late = (cotangent, out_gain, out_bias, out_weight)
+    sources = (pair_hbm, *weights_hbm[:5], cotangent_hbm, *weights_hbm[5:])
+    loads = [
+        pltpu.make_async_copy(src, dst, load_sem.at[t])
+        for t, (src, dst) in enumerate(zip(sources, early + late))
+    ]
+    for load in loads:
+        load.start()
     barrier = pltpu.get_barrier_semaphore()
-
-    def greet(d, carry):
-        peer = lax.rem(me + d, n)
-        pl.semaphore_signal(barrier, inc=1, device_id=coords(peer), device_id_type=MESH)
-        return carry
+    others = peers(row, col)
+    for to_row, to_col, _ in others:
+        pl.semaphore_signal(barrier, inc=1, device_id=(to_row, to_col), device_id_type=MESH)
 
     def start_all(phase, src, dst, same=False):
-        def send(d, carry):
-            peer = lax.rem(me + d, n)
+        for to_row, to_col, peer in others:
             pltpu.make_async_remote_copy(
                 src_ref=src if same else src.at[peer],
                 dst_ref=dst.at[me],
                 send_sem=send_sem.at[phase],
                 recv_sem=recv_sem.at[phase],
-                device_id=coords(peer),
+                device_id=(to_row, to_col),
                 device_id_type=MESH,
             ).start()
-            return carry
-
-        lax.fori_loop(1, n, send, 0)
         dst[me] = src[...] if same else src[me]
 
     def wait_on(sems, phase, dst):
-        others = dst.at[pl.ds(0, n - 1)]
-        pltpu.make_async_copy(others, others, sems.at[phase]).wait()
+        part = dst.at[pl.ds(0, n - 1)]
+        pltpu.make_async_copy(part, part, sems.at[phase]).wait()
 
     def pack(dst, count, stride):
         def body(h, carry):
@@ -208,8 +251,8 @@
                 dst[r * n_col + 2 * q, at : at + half, :] = a.astype(BF)
                 dst[r * n_col + 2 * q + 1, at : at + half, :] = b.astype(BF)
 
-    lax.fori_loop(1, n, greet, 0)
-
+    for load in loads[: len(early)]:
+        load.wait()
     gain = column(norm_gain)
     bias = column(norm_bias)
     forward_weight = jnp.concatenate(
@@ -257,6 +300,8 @@
     disassemble(dot_last(big_l[...], big_r[...]), send_b, 0)
     start_all(1, send_b, recv_b)
 
+    for load in loads[len(early) :]:
+        load.wait()
     o_gain = column(out_gain)
     o_bias = column(out_bias)
     out_back = out_weight[...]
@@ -359,14 +404,49 @@
     send_f[...] = (total * (1.0 / tokens)).astype(BF)
     start_all(5, send_f, recv_f, same=True)
     wait_on(recv_sem, 5, recv_f)
-    unpack(recv_f, 8, 24)
-    grad_left[...] = collect(0, 24, 2)
-    grad_right[...] = collect(2, 24, 2)
-    grad_gating[...] = collect(4, 24, 1)
-    grad_output[...] = collect(5, 24, 1)
-    grad_norms[...] = jnp.transpose(collect(6, 24, 1))[:4]
     for phase, dst in enumerate((recv_a, recv_b, recv_c, recv_d, recv_e, recv_f)):
         wait_on(send_sem, phase, dst)
+
+
+def finish(
+    update_in,
+    grad_pair_in,
+    totals,
+    update,
+    grad_pair,
+    grad_left,
+    grad_right,
+    grad_gating,
+    grad_output,
+    grad_norms,
+    stage,
+    sems,
+):
+    stores = [
+        pltpu.make_async_copy(update_in, update, sems.at[0]),
+        pltpu.make_async_copy(grad_pair_in, grad_pair, sems.at[1]),
+    ]
+    for store in stores:
+        store.start()
+
+    def unpack(h, carry):
+        at = pl.multiple_of(h * 24, 8)
+        stage[pl.ds(at, 8), :] = totals[h].astype(F32)
+        return carry
+
+    lax.fori_loop(0, LANES, unpack, 0, unroll=8)
+
+    def collect(first):
+        return stage[pl.ds(first, LANES, stride=24), :]
+
+    for t in range(2):
+        grad_left[:, t * LANES : (t + 1) * LANES] = collect(t)
+        grad_right[:, t * LANES : (t + 1) * LANES] = collect(2 + t)
+    grad_gating[...] = collect(4)
+    grad_output[...] = collect(5)
+    grad_norms[...] = jnp.transpose(collect(6))[:4]
+    for store in stores:
+        store.wait()
 
 
 def per_device(pair, cotangent, length, *weights):
@@ -382,20 +462,22 @@
     vmem = pl.BlockSpec(memory_space=pltpu.VMEM)
     smem = pl.BlockSpec(memory_space=pltpu.SMEM)
     shape = jax.ShapeDtypeStruct
-    return pl.pallas_call(
+    hbm = pl.BlockSpec(memory_space=pl.ANY)
+    far = functools.partial(pltpu.with_memory_space_constraint, memory_space=pltpu.HBM)
+    raw = pl.pallas_call(
         functools.partial(kernel, n_row, n_col),
         out_shape=(
-            shape(pair.shape, BF),
-            shape(pair.shape, BF),
-            shape((chan, 2 * hidden), F32),
-            shape((chan, 2 * hidden), F32),
-            shape((chan, chan), F32),
-            shape((hidden, chan), F32),
-            shape((4, chan), F32),
+            pltpu.VMEM(pair.shape, BF),
+            pltpu.VMEM(pair.shape, BF),
+            pltpu.VMEM((n, 8, LANES), BF),
         ),
-        in_specs=[vmem, vmem, smem] + [vmem] * len(weights),
-        out_specs=(vmem,) * 7,
+        in_specs=[hbm, hbm, smem] + [hbm] * len(weights),
+        out_specs=(vmem,) * 3,
         scratch_shapes=[
+            pltpu.VMEM(pair.shape, BF),
+            *[pltpu.VMEM(w.shape, w.dtype) for w in weights[:5]],
+            pltpu.VMEM(pair.shape, BF),
+            *[pltpu.VMEM(w.shape, w.dtype) for w in weights[5:]],
             pltpu.VMEM((n * 40, LANES), F32),
             pltpu.VMEM((chan, places), F32),
             pltpu.VMEM((1, places), F32),
@@ -421,15 +503,33 @@
             pltpu.VMEM((n, 8, LANES), BF),
             pltpu.VMEM((n, 8, LANES), BF),
             pltpu.VMEM((8, LANES), BF),
-            pltpu.VMEM((n, 8, LANES), BF),
             pltpu.SemaphoreType.DMA((6,)),
             pltpu.SemaphoreType.DMA((6,)),
+            pltpu.SemaphoreType.DMA((10,)),
         ],
         compiler_params=pltpu.CompilerParams(
-            collective_id=0, has_side_effects=True, vmem_limit_bytes=56 << 20
+            collective_id=0, has_side_effects=True, vmem_limit_bytes=40 << 20
         ),
         name="triangle",
-    )(pair, cotangent, length, *weights)
+    )(far(pair), far(cotangent), length, *[far(w) for w in weights])
+    raw = [pltpu.with_memory_space_constraint(a, pltpu.VMEM) for a in raw]
+    return pl.pallas_call(
+        finish,
+        out_shape=(
+            shape(pair.shape, BF),
+            shape(pair.shape, BF),
+            shape((chan, 2 * hidden), F32),
+            shape((chan, 2 * hidden), F32),
+            shape((chan, chan), F32),
+            shape((hidden, chan), F32),
+            shape((4, chan), F32),
+        ),
+        in_specs=[vmem] * 3,
+        out_specs=(hbm, hbm) + (vmem,) * 5,
+        scratch_shapes=[pltpu.VMEM((LANES * 24, LANES), F32), pltpu.SemaphoreType.DMA((2,))],
+        compiler_params=pltpu.CompilerParams(vmem_limit_bytes=8 << 20),
+        name="finish",
+    )(*raw)
 
 
 def solution(mesh):

time: 102 us -> 82.3 us (0.81)
  Pallas kernels: 92.3 us -> 79.7 us
  local copies, waits for them, and re-layouts: 6.88 us -> 0 us
    pallas_call x1 -> x2, Pallas kernels: 92.3 us -> 79.7 us  [the longest x1 78 us: per_device(): pl.pallas_call(functools.partial(kernel, n_row, n_col), out_shape=(pltpu....]
    unnamed x19 -> x0, local copies, waits for them, and re-layouts: 6.88 us -> none
where the time goes in v5:
time: 82.3 us; the launch traced here: 81 us
  Pallas kernels  79.7 us (97%)
  between operations  1.29 us (2%)
    pallas_call x1, Pallas kernels, per_device(): pl.pallas_call(functools.partial(kernel, n_row, n_col), out_shape=(pltpu....  78 us
    pallas_call x1, Pallas kernels, per_device(): pl.pallas_call(finish, out_shape=(shape(pair.shape, BF), shape(pair.shape...  1.72 us

profile of v5, /device:TPU:0, one launch (start us, length us, event | category | flops | bytes accessed | tf_op | source)
XLA Modules:
  0.0 81.0 jit_solution(16708168192299503564)
XLA Ops:
  1.3 78.0 %triangle.1 = (bf16[32,64,128]{2,1,0:T(8,128)(2,1)S(1)}, bf16[32,64,128]{2,1,0:T(8,128)(2,1)S(1)}, bf16[128,8,128]{2,1,0:T(8,128)(2,1)S(1)}) custom-call(bf16[32,64,128]{2,1,0:T(8,128)(2,1)} %pair_hbm.1, bf16[32,64,128]{2,1,0:T(8,128)(2,1)} %cotangent_hbm.1, s32[1]{0:T(128)S(6)} %copy.18.length, f32[1,128]{1,0:T(1,128)} %bitcast.4, f32[1,128]{1,0:T(1,128)} %bitcast.5, ...), custom_call_target="tpu_custom_call" | custom-call | tf_op jit(solution)/shard_map/triangle/pallas_call | solution.py:467
  79.3 1.7 %finish.1 = (bf16[32,64,128]{2,1,0:T(8,128)(2,1)}, bf16[32,64,128]{2,1,0:T(8,128)(2,1)}, f32[128,256]{1,0:T(8,128)}, f32[128,256]{1,0:T(8,128)}, f32[128,128]{1,...) custom-call(bf16[32,64,128]{2,1,0:T(8,128)(2,1)S(1)} %get-tuple-element.10.update_in, ...), custom_call_target="tpu_custom_call" | custom-call | tf_op jit(solution)/shard_map/finish/pallas_call | solution.py:516

commit v6 on v5

--- a/solution.py
+++ b/solution.py
@@ -124,6 +124,9 @@
     normed_s,
     coef_s,
     gate_s,
+    up_s,
+    hgrad_s,
+    that_s,
     tnormed_s,
     ograd_s,
     ggrad_s,
@@ -134,12 +137,16 @@
     big_g,
     send_a,
     recv_a,
+    send_l,
+    recv_l,
     send_b,
     recv_b,
     send_c,
     recv_c,
-    send_d,
-    recv_d,
+    send_row,
+    recv_row,
+    send_col,
+    recv_col,
     send_e,
     recv_e,
     send_f,
@@ -154,6 +161,8 @@
     tokens = n_row * rows
     half = rows // 2
     wide = GROUP * LANES
+    part = blocks // 2
+    groups = part // GROUP
     row = lax.axis_index("row")
     col = lax.axis_index("col")
     me = row * n_col + col
@@ -185,20 +194,20 @@
         dst[me] = src[...] if same else src[me]
 
     def wait_on(sems, phase, dst):
-        part = dst.at[pl.ds(0, n - 1)]
-        pltpu.make_async_copy(part, part, sems.at[phase]).wait()
-
-    def pack(dst, count, stride):
+        blocks_of = dst.at[pl.ds(0, n - 1)]
+        pltpu.make_async_copy(blocks_of, blocks_of, sems.at[phase]).wait()
+
+    def pack(dst, count, stride, first=0):
         def body(h, carry):
-            at = pl.multiple_of(h * stride, 8)
+            at = pl.multiple_of(h * stride + first, 8)
             dst[h] = stage[pl.ds(at, count), :].astype(BF)
             return carry
 
         lax.fori_loop(0, n, body, 0, unroll=8)
 
-    def unpack(src, count, stride):
+    def unpack(src, count, stride, first=0):
         def body(h, carry):
-            at = pl.multiple_of(h * stride, 8)
+            at = pl.multiple_of(h * stride + first, 8)
             stage[pl.ds(at, count), :] = src[h].astype(F32)
             return carry
 
@@ -229,27 +238,25 @@
     def lanes_at(first):
         return pl.ds(pl.multiple_of(first * LANES, LANES), wide)
 
-    def assemble(src, at, dst):
+    def assemble(src, at, count, dst):
         def body(r, carry):
             for q in range(n_col // 2):
-                a = src[r * n_col + 2 * q, at : at + half, :].astype(F32)
-                b = src[r * n_col + 2 * q + 1, at : at + half, :].astype(F32)
-                low, high = halves(a, b)
-                base = pl.multiple_of(r * rows, rows)
-                dst[pl.ds(base, half), q * LANES : (q + 1) * LANES] = low.astype(BF)
-                dst[pl.ds(base + half, half), q * LANES : (q + 1) * LANES] = high.astype(BF)
+                a = src[r * n_col + 2 * q, at : at + count, :].astype(F32)
+                b = src[r * n_col + 2 * q + 1, at : at + count, :].astype(F32)
+                both = jnp.concatenate(halves(a, b), axis=0).astype(BF)
+                base = pl.multiple_of(r * 2 * count, 2 * count)
+                dst[pl.ds(base, 2 * count), q * LANES : (q + 1) * LANES] = both
             return carry
 
         lax.fori_loop(0, n_row, body, 0, unroll=2)
 
-    def disassemble(values, dst, at):
+    def disassemble(values, count, dst):
         for r in range(n_row):
             for q in range(n_col // 2):
-                low = values[r * rows : r * rows + half, q * LANES : (q + 1) * LANES]
-                high = values[r * rows + half : (r + 1) * rows, q * LANES : (q + 1) * LANES]
-                a, b = halves(low, high)
-                dst[r * n_col + 2 * q, at : at + half, :] = a.astype(BF)
-                dst[r * n_col + 2 * q + 1, at : at + half, :] = b.astype(BF)
+                block = values[r * 2 * count : (r + 1) * 2 * count, q * LANES : (q + 1) * LANES]
+                a, b = halves(block[:count], block[count:])
+                dst[r * n_col + 2 * q] = a.astype(BF)
+                dst[r * n_col + 2 * q + 1] = b.astype(BF)
 
     for load in loads[: len(early)]:
         load.wait()
@@ -285,20 +292,16 @@
             act = sig * proj[base : base + hidden]
             coef_s[2 * side, :, at] = sig
             coef_s[2 * side + 1, :, at] = act * (1.0 - sig)
-            spread(act, first + side * blocks, 40)
+            spread(act, first + (1 - side) * blocks, 40)
         gate_s[:, at] = jax.nn.sigmoid(proj[4 * hidden :])
         return carry
 
     lax.fori_loop(0, blocks // GROUP, first_pass, 0)
-    pack(send_a, 2 * blocks, 40)
+    pack(send_a, blocks + part, 40)
+    pack(send_l, part, 40, blocks + part)
     pl.semaphore_wait(barrier, n - 1)
     start_all(0, send_a, recv_a)
-
-    wait_on(recv_sem, 0, recv_a)
-    assemble(recv_a, 0, big_l)
-    assemble(recv_a, blocks, big_r)
-    disassemble(dot_last(big_l[...], big_r[...]), send_b, 0)
-    start_all(1, send_b, recv_b)
+    start_all(1, send_l, recv_l)
 
     for load in loads[len(early) :]:
         load.wait()
@@ -306,65 +309,95 @@
     o_bias = column(out_bias)
     out_back = out_weight[...]
     out_forward = jnp.transpose(out_back)
-    wait_on(recv_sem, 1, recv_b)
-    unpack(recv_b, blocks, 24)
-
-    def second_pass(g, carry):
+    zero = jnp.zeros((hidden, 1), F32)
+
+    def early_pass(g, carry):
         first = g * GROUP
         at = lanes_at(first)
-        hat, scale = center_scale(collect(first, 24, GROUP))
+        upstream = channels_first(cotangent, first)
+        up_s[:, at] = upstream.astype(BF)
+        outer_grad = (upstream * gate_s[:, at]).astype(BF)
+        ograd_s[:, at] = outer_grad
+        tnorm_grad = dot(out_back, outer_grad)
+        hgrad_s[:, at] = tnorm_grad
+        return carry + jnp.sum(tnorm_grad, axis=1, keepdims=True)
+
+    o_bias_grad = lax.fori_loop(0, blocks // GROUP, early_pass, zero)
+
+    wait_on(recv_sem, 0, recv_a)
+    assemble(recv_a, 0, blocks, big_r)
+    assemble(recv_a, blocks, part, big_l.at[0])
+    disassemble(dot_last(big_l[0], big_r[...]), part, send_b.at[0])
+    start_all(2, send_b.at[0], recv_b.at[0])
+    wait_on(recv_sem, 1, recv_l)
+    assemble(recv_l, 0, part, big_l.at[1])
+    disassemble(dot_last(big_l[1], big_r[...]), part, send_b.at[1])
+    start_all(3, send_b.at[1], recv_b.at[1])
+
+    for piece in range(2):
+        wait_on(recv_sem, 2 + piece, recv_b.at[piece])
+        unpack(recv_b.at[piece], part, 24)
+
+        def second_pass(g, carry):
+            first = g * GROUP
+            at = lanes_at(piece * part + first)
+            hat, scale = center_scale(collect(first, 24, GROUP))
+            that_s[:, at] = hat
+            spread(norm_back(hgrad_s[:, at] * o_gain, hat, scale), first, 24)
+            return carry
+
+        lax.fori_loop(0, groups, second_pass, 0)
+        pack(send_c.at[piece], part, 24)
+        start_all(4 + piece, send_c.at[piece], recv_c.at[piece])
+
+    def late_pass(g, carry):
+        first = g * GROUP
+        at = lanes_at(first)
+        hat = that_s[:, at]
         tri_normed = (hat * o_gain + o_bias).astype(BF)
         tnormed_s[:, at] = tri_normed
-        outer = dot(out_forward, tri_normed)
         gate = gate_s[:, at]
-        gated = gate * outer
+        gated = gate * dot(out_forward, tri_normed)
         positions_first(update, first, gated)
-        upstream = channels_first(cotangent, first)
-        outer_grad = (upstream * gate).astype(BF)
-        ograd_s[:, at] = outer_grad
-        ggrad_s[:, at] = (upstream * gated * (1.0 - gate)).astype(BF)
-        tnorm_grad = dot(out_back, outer_grad)
-        spread(norm_back(tnorm_grad * o_gain, hat, scale), first, 24)
-        along = tnorm_grad * hat
-        return (
-            carry[0] + jnp.sum(along, axis=1, keepdims=True),
-            carry[1] + jnp.sum(tnorm_grad, axis=1, keepdims=True),
-        )
-
-    zero = jnp.zeros((hidden, 1), F32)
-    o_gain_grad, o_bias_grad = lax.fori_loop(0, blocks // GROUP, second_pass, (zero, zero))
-    pack(send_c, blocks, 24)
-    start_all(2, send_c, recv_c)
+        ggrad_s[:, at] = (up_s[:, at].astype(F32) * gated * (1.0 - gate)).astype(BF)
+        return carry + jnp.sum(hgrad_s[:, at] * hat, axis=1, keepdims=True)
+
+    o_gain_grad = lax.fori_loop(0, blocks // GROUP, late_pass, zero)
     back_s[...] = dot(gate_weight[...], ggrad_s[...])
     part_output = dot_last(tnormed_s[...], ograd_s[...])
     part_gating = dot_last(normed_s[...], ggrad_s[...])
 
-    wait_on(recv_sem, 2, recv_c)
-    assemble(recv_c, 0, big_g)
-    disassemble(dot(big_g[...], big_r[...]), send_d, 0)
-    disassemble(dot_first(big_g[...], big_l[...]), send_d, blocks)
-    start_all(3, send_d, recv_d)
-
-    backward_weight = jnp.concatenate([left_weight[...], right_weight[...]], axis=1)
-    wait_on(recv_sem, 3, recv_d)
-    unpack(recv_d, 2 * blocks, 40)
-
-    def third_pass(g, carry):
+    for piece in range(2):
+        wait_on(recv_sem, 4 + piece, recv_c.at[piece])
+        here = pl.ds(piece * tokens // 2, tokens // 2)
+        assemble(recv_c.at[piece], 0, part, big_g.at[here])
+        disassemble(dot(big_g[here], big_r[...]), part, send_row.at[piece])
+        start_all(6 + piece, send_row.at[piece], recv_row.at[piece])
+    all_l = jnp.concatenate([big_l[0], big_l[1]], axis=0)
+    disassemble(dot_first(big_g[...], all_l), blocks, send_col)
+    start_all(8, send_col, recv_col)
+
+    for piece in range(2):
+        wait_on(recv_sem, 6 + piece, recv_row.at[piece])
+        unpack(recv_row.at[piece], part, 24, piece * part)
+
+    def through(weight, side, g):
         first = g * GROUP
         at = lanes_at(first)
-        from_row = collect(first, 40, GROUP)
-        from_col = collect(first + blocks, 40, GROUP)
+        grad = collect(first, 24, GROUP)
         comb = jnp.concatenate(
-            [
-                from_row * coef_s[0, :, at],
-                from_row * coef_s[1, :, at],
-                from_col * coef_s[2, :, at],
-                from_col * coef_s[3, :, at],
-            ],
-            axis=0,
+            [grad * coef_s[2 * side, :, at], grad * coef_s[2 * side + 1, :, at]], axis=0
         ).astype(BF)
-        comb_s[:, at] = comb
-        normed_grad = back_s[:, at] + dot(backward_weight, comb)
+        comb_s[2 * hidden * side : 2 * hidden * (side + 1), at] = comb
+        return at, back_s[:, at] + dot(weight[...], comb)
+
+    def row_pass(g, carry):
+        at, normed_grad = through(left_weight, 0, g)
+        back_s[:, at] = normed_grad
+        return carry
+
+    def col_pass(g, carry):
+        at, normed_grad = through(right_weight, 1, g)
         back_s[:, at] = normed_grad
         along = normed_grad * hat_s[:, at]
         return (
@@ -372,8 +405,13 @@
             carry[1] + jnp.sum(normed_grad, axis=1, keepdims=True),
         )
 
-    gain_grad, bias_grad = lax.fori_loop(0, blocks // GROUP, third_pass, (zero, zero))
-    spread(dot_last(normed_s[...], comb_s[...]), 0, 24)
+    lax.fori_loop(0, blocks // GROUP, row_pass, 0)
+    part_left = dot_last(normed_s[...], comb_s[: 2 * hidden])
+    wait_on(recv_sem, 8, recv_col)
+    unpack(recv_col, blocks, 24)
+    gain_grad, bias_grad = lax.fori_loop(0, blocks // GROUP, col_pass, (zero, zero))
+    spread(part_left, 0, 24)
+    spread(dot_last(normed_s[...], comb_s[2 * hidden :]), 2, 24)
     spread(part_gating, 4, 24)
     spread(part_output, 5, 24)
     lane = lax.broadcasted_iota(jnp.int32, (LANES, LANES), 1)
@@ -384,7 +422,7 @@
     spread(norms, 6, 24)
     spread(jnp.zeros_like(norms), 7, 24)
     pack(send_e, 8, 24)
-    start_all(4, send_e, recv_e)
+    start_all(9, send_e, recv_e)
 
     def fourth_pass(g, carry):
         first = g * GROUP
@@ -395,16 +433,17 @@
 
     lax.fori_loop(0, blocks // GROUP, fourth_pass, 0)
 
-    wait_on(recv_sem, 4, recv_e)
+    wait_on(recv_sem, 9, recv_e)
 
     def add(p, total):
         return total + recv_e[p].astype(F32)
 
     total = lax.fori_loop(0, n, add, jnp.zeros((8, LANES), F32), unroll=8)
     send_f[...] = (total * (1.0 / tokens)).astype(BF)
-    start_all(5, send_f, recv_f, same=True)
-    wait_on(recv_sem, 5, recv_f)
-    for phase, dst in enumerate((recv_a, recv_b, recv_c, recv_d, recv_e, recv_f)):
+    start_all(10, send_f, recv_f, same=True)
+    wait_on(recv_sem, 10, recv_f)
+    halved = [dst.at[piece] for dst in (recv_b, recv_c, recv_row) for piece in range(2)]
+    for phase, dst in enumerate((recv_a, recv_l, *halved, recv_col, recv_e, recv_f)):
         wait_on(send_sem, phase, dst)
 
 
@@ -458,6 +497,7 @@
     tokens = n_row * rows
     places = rows * cols
     blocks = places // LANES
+    part = blocks // 2
     weights = [w.reshape(1, -1) if w.ndim == 1 else w for w in weights]
     vmem = pl.BlockSpec(memory_space=pltpu.VMEM)
     smem = pl.BlockSpec(memory_space=pltpu.SMEM)
@@ -484,27 +524,25 @@
             pltpu.VMEM((chan, places), BF),
             pltpu.VMEM((4, hidden, places), F32),
             pltpu.VMEM((chan, places), F32),
+            pltpu.VMEM((chan, places), BF),
+            pltpu.VMEM((hidden, places), F32),
+            pltpu.VMEM((hidden, places), F32),
             pltpu.VMEM((hidden, places), BF),
             pltpu.VMEM((chan, places), BF),
             pltpu.VMEM((chan, places), BF),
             pltpu.VMEM((chan, places), F32),
             pltpu.VMEM((4 * hidden, places), BF),
+            pltpu.VMEM((2, tokens // 2, tokens), BF),
             pltpu.VMEM((tokens, tokens), BF),
             pltpu.VMEM((tokens, tokens), BF),
-            pltpu.VMEM((tokens, tokens), BF),
-            pltpu.VMEM((n, 2 * blocks, LANES), BF),
-            pltpu.VMEM((n, 2 * blocks, LANES), BF),
-            pltpu.VMEM((n, blocks, LANES), BF),
-            pltpu.VMEM((n, blocks, LANES), BF),
-            pltpu.VMEM((n, blocks, LANES), BF),
-            pltpu.VMEM((n, blocks, LANES), BF),
-            pltpu.VMEM((n, 2 * blocks, LANES), BF),
-            pltpu.VMEM((n, 2 * blocks, LANES), BF),
-            pltpu.VMEM((n, 8, LANES), BF),
-            pltpu.VMEM((n, 8, LANES), BF),
+            *[pltpu.VMEM((n, blocks + part, LANES), BF)] * 2,
+            *[pltpu.VMEM((n, part, LANES), BF)] * 2,
+            *[pltpu.VMEM((2, n, part, LANES), BF)] * 6,
+            *[pltpu.VMEM((n, blocks, LANES), BF)] * 2,
+            *[pltpu.VMEM((n, 8, LANES), BF)] * 2,
             pltpu.VMEM((8, LANES), BF),
-            pltpu.SemaphoreType.DMA((6,)),
-            pltpu.SemaphoreType.DMA((6,)),
+            pltpu.SemaphoreType.DMA((11,)),
+            pltpu.SemaphoreType.DMA((11,)),
             pltpu.SemaphoreType.DMA((10,)),
         ],
         compiler_params=pltpu.CompilerParams(

time: 82.3 us -> 75.1 us (0.913)
  Pallas kernels: 79.7 us -> 72.6 us
    pallas_call x1, Pallas kernels: 78 us -> 70.9 us  [per_device(): pl.pallas_call(functools.partial(kernel, n_row, n_col), out_shape=(pltpu....]
where the time goes in v6:
time: 75.1 us; the launch traced here: 73.9 us
  Pallas kernels  72.6 us (97%)
  between operations  1.29 us (2%)
    pallas_call x1, Pallas kernels, per_device(): pl.pallas_call(functools.partial(kernel, n_row, n_col), out_shape=(pltpu....  70.9 us
    pallas_call x1, Pallas kernels, per_device(): pl.pallas_call(finish, out_shape=(shape(pair.shape, BF), shape(pair.shape...  1.72 us

profile of v6, /device:TPU:0, one launch (start us, length us, event | category | flops | bytes accessed | tf_op | source)
XLA Modules:
  0.0 73.9 jit_solution(14245328002422516702)
XLA Ops:
  1.3 70.9 %triangle.1 = (bf16[32,64,128]{2,1,0:T(8,128)(2,1)S(1)}, bf16[32,64,128]{2,1,0:T(8,128)(2,1)S(1)}, bf16[128,8,128]{2,1,0:T(8,128)(2,1)S(1)}) custom-call(bf16[32,64,128]{2,1,0:T(8,128)(2,1)} %pair_hbm.1, bf16[32,64,128]{2,1,0:T(8,128)(2,1)} %cotangent_hbm.1, s32[1]{0:T(128)S(6)} %copy.18.length, f32[1,128]{1,0:T(1,128)} %bitcast.4, f32[1,128]{1,0:T(1,128)} %bitcast.5, ...), custom_call_target="tpu_custom_call" | custom-call | tf_op jit(solution)/shard_map/triangle/pallas_call | solution.py:507
  72.2 1.7 %finish.1 = (bf16[32,64,128]{2,1,0:T(8,128)(2,1)}, bf16[32,64,128]{2,1,0:T(8,128)(2,1)}, f32[128,256]{1,0:T(8,128)}, f32[128,256]{1,0:T(8,128)}, f32[128,128]{1,...) custom-call(bf16[32,64,128]{2,1,0:T(8,128)(2,1)S(1)} %get-tuple-element.10.update_in, ...), custom_call_target="tpu_custom_call" | custom-call | tf_op jit(solution)/shard_map/finish/pallas_call | solution.py:554

commit v7 on v6

--- a/solution.py
+++ b/solution.py
@@ -12,7 +12,7 @@
 BF = jnp.bfloat16
 F32 = jnp.float32
 LANES = 128
-GROUP = 4
+GROUP = 8
 
 
 def dot(a, b):
@@ -107,7 +107,11 @@
     weights_hbm,
     update,
     grad_pair,
-    recv_f,
+    grad_left,
+    grad_right,
+    grad_gating,
+    grad_output,
+    grad_norms,
     pair,
     norm_gain,
     norm_bias,
@@ -135,8 +139,8 @@
     big_l,
     big_r,
     big_g,
-    send_a,
-    recv_a,
+    send_r,
+    recv_r,
     send_l,
     recv_l,
     send_b,
@@ -149,7 +153,12 @@
     recv_col,
     send_e,
     recv_e,
+    send_h,
+    recv_h,
     send_f,
+    recv_f,
+    send_g,
+    recv_g,
     send_sem,
     recv_sem,
     load_sem,
@@ -297,11 +306,13 @@
         return carry
 
     lax.fori_loop(0, blocks // GROUP, first_pass, 0)
-    pack(send_a, blocks + part, 40)
-    pack(send_l, part, 40, blocks + part)
+    pack(send_r, blocks, 40)
+    for piece in range(2):
+        pack(send_l.at[piece], part, 40, blocks + piece * part)
     pl.semaphore_wait(barrier, n - 1)
-    start_all(0, send_a, recv_a)
-    start_all(1, send_l, recv_l)
+    start_all(0, send_r, recv_r)
+    for piece in range(2):
+        start_all(1 + piece, send_l.at[piece], recv_l.at[piece])
 
     for load in loads[len(early) :]:
         load.wait()
@@ -324,18 +335,16 @@
 
     o_bias_grad = lax.fori_loop(0, blocks // GROUP, early_pass, zero)
 
-    wait_on(recv_sem, 0, recv_a)
-    assemble(recv_a, 0, blocks, big_r)
-    assemble(recv_a, blocks, part, big_l.at[0])
-    disassemble(dot_last(big_l[0], big_r[...]), part, send_b.at[0])
-    start_all(2, send_b.at[0], recv_b.at[0])
-    wait_on(recv_sem, 1, recv_l)
-    assemble(recv_l, 0, part, big_l.at[1])
-    disassemble(dot_last(big_l[1], big_r[...]), part, send_b.at[1])
-    start_all(3, send_b.at[1], recv_b.at[1])
-
+    wait_on(recv_sem, 0, recv_r)
+    assemble(recv_r, 0, blocks, big_r)
     for piece in range(2):
-        wait_on(recv_sem, 2 + piece, recv_b.at[piece])
+        wait_on(recv_sem, 1 + piece, recv_l.at[piece])
+        assemble(recv_l.at[piece], 0, part, big_l.at[piece])
+        disassemble(dot_last(big_l[piece], big_r[...]), part, send_b.at[piece])
+        start_all(3 + piece, send_b.at[piece], recv_b.at[piece])
+
+    for piece in range(2):
+        wait_on(recv_sem, 3 + piece, recv_b.at[piece])
         unpack(recv_b.at[piece], part, 24)
 
         def second_pass(g, carry):
@@ -348,7 +357,7 @@
 
         lax.fori_loop(0, groups, second_pass, 0)
         pack(send_c.at[piece], part, 24)
-        start_all(4 + piece, send_c.at[piece], recv_c.at[piece])
+        start_all(5 + piece, send_c.at[piece], recv_c.at[piece])
 
     def late_pass(g, carry):
         first = g * GROUP
@@ -368,61 +377,84 @@
     part_gating = dot_last(normed_s[...], ggrad_s[...])
 
     for piece in range(2):
-        wait_on(recv_sem, 4 + piece, recv_c.at[piece])
+        wait_on(recv_sem, 5 + piece, recv_c.at[piece])
         here = pl.ds(piece * tokens // 2, tokens // 2)
         assemble(recv_c.at[piece], 0, part, big_g.at[here])
         disassemble(dot(big_g[here], big_r[...]), part, send_row.at[piece])
-        start_all(6 + piece, send_row.at[piece], recv_row.at[piece])
+        start_all(7 + piece, send_row.at[piece], recv_row.at[piece])
     all_l = jnp.concatenate([big_l[0], big_l[1]], axis=0)
-    disassemble(dot_first(big_g[...], all_l), blocks, send_col)
-    start_all(8, send_col, recv_col)
-
+    col_own = dot_first(big_g[...], all_l)
+    for r in range(n_row):
+        for q in range(n_col // 2):
+            block = col_own[r * rows : (r + 1) * rows, q * LANES : (q + 1) * LANES]
+            for t, tile in enumerate(halves(block[:half], block[half:])):
+                for piece in range(2):
+                    send_col[piece, r * n_col + 2 * q + t] = tile[
+                        piece * part : (piece + 1) * part
+                    ].astype(BF)
     for piece in range(2):
-        wait_on(recv_sem, 6 + piece, recv_row.at[piece])
-        unpack(recv_row.at[piece], part, 24, piece * part)
-
-    def through(weight, side, g):
-        first = g * GROUP
-        at = lanes_at(first)
-        grad = collect(first, 24, GROUP)
-        comb = jnp.concatenate(
-            [grad * coef_s[2 * side, :, at], grad * coef_s[2 * side + 1, :, at]], axis=0
-        ).astype(BF)
-        comb_s[2 * hidden * side : 2 * hidden * (side + 1), at] = comb
-        return at, back_s[:, at] + dot(weight[...], comb)
-
-    def row_pass(g, carry):
-        at, normed_grad = through(left_weight, 0, g)
-        back_s[:, at] = normed_grad
-        return carry
-
-    def col_pass(g, carry):
-        at, normed_grad = through(right_weight, 1, g)
-        back_s[:, at] = normed_grad
-        along = normed_grad * hat_s[:, at]
-        return (
-            carry[0] + jnp.sum(along, axis=1, keepdims=True),
-            carry[1] + jnp.sum(normed_grad, axis=1, keepdims=True),
-        )
-
-    lax.fori_loop(0, blocks // GROUP, row_pass, 0)
-    part_left = dot_last(normed_s[...], comb_s[: 2 * hidden])
-    wait_on(recv_sem, 8, recv_col)
-    unpack(recv_col, blocks, 24)
-    gain_grad, bias_grad = lax.fori_loop(0, blocks // GROUP, col_pass, (zero, zero))
-    spread(part_left, 0, 24)
-    spread(dot_last(normed_s[...], comb_s[2 * hidden :]), 2, 24)
-    spread(part_gating, 4, 24)
-    spread(part_output, 5, 24)
+        start_all(9 + piece, send_col.at[piece], recv_col.at[piece])
+
+    def through(side, piece, phase, recv, weight):
+        wait_on(recv_sem, phase + piece, recv.at[piece])
+        unpack(recv.at[piece], part, 24)
+        lines = slice(2 * hidden * side, 2 * hidden * (side + 1))
+
+        def one(g, carry):
+            first = g * GROUP
+            at = lanes_at(piece * part + first)
+            grad = collect(first, 24, GROUP)
+            comb = jnp.concatenate(
+                [grad * coef_s[2 * side, :, at], grad * coef_s[2 * side + 1, :, at]], axis=0
+            ).astype(BF)
+            comb_s[lines, at] = comb
+            normed_grad = back_s[:, at] + dot(weight[...], comb)
+            back_s[:, at] = normed_grad
+            if side == 0:
+                return carry
+            along = normed_grad * hat_s[:, at]
+            return (
+                carry[0] + jnp.sum(along, axis=1, keepdims=True),
+                carry[1] + jnp.sum(normed_grad, axis=1, keepdims=True),
+            )
+
+        sums = lax.fori_loop(0, groups, one, (zero, zero))
+        held = slice(piece * part * LANES, (piece + 1) * part * LANES)
+        return dot_last(normed_s[:, held], comb_s[lines, held]), sums
+
     lane = lax.broadcasted_iota(jnp.int32, (LANES, LANES), 1)
-    norms = jnp.where(lane == 0, gain_grad, 0.0)
-    norms = jnp.where(lane == 1, bias_grad, norms)
-    norms = jnp.where(lane == 2, o_gain_grad, norms)
-    norms = jnp.where(lane == 3, o_bias_grad, norms)
-    spread(norms, 6, 24)
-    spread(jnp.zeros_like(norms), 7, 24)
-    pack(send_e, 8, 24)
-    start_all(9, send_e, recv_e)
+
+    def side_by_side(*columns):
+        both = jnp.zeros((LANES, LANES), F32)
+        for t, values in enumerate(columns):
+            both = jnp.where(lane == t, values, both)
+        return both
+
+    def sum_up(recv):
+        def add(p, total):
+            return total + recv[p].astype(F32)
+
+        zeros = jnp.zeros(recv.shape[1:], F32)
+        return (lax.fori_loop(0, n, add, zeros, unroll=8) * (1.0 / tokens)).astype(BF)
+
+    left_0, _ = through(0, 0, 7, recv_row, left_weight)
+    left_1, _ = through(0, 1, 7, recv_row, left_weight)
+    spread(left_0 + left_1, 0, 24)
+    spread(part_gating, 2, 24)
+    spread(part_output, 3, 24)
+    pack(send_e, 4, 24)
+    start_all(11, send_e, recv_e)
+    right_0, sums_0 = through(1, 0, 9, recv_col, right_weight)
+    right_1, sums_1 = through(1, 1, 9, recv_col, right_weight)
+    spread(right_0 + right_1, 0, 24)
+    gain_grad, bias_grad = sums_0[0] + sums_1[0], sums_0[1] + sums_1[1]
+    spread(side_by_side(gain_grad, bias_grad, o_gain_grad, o_bias_grad), 2, 24)
+    pack(send_h, 4, 24)
+    start_all(12, send_h, recv_h)
+
+    wait_on(recv_sem, 11, recv_e)
+    send_f[...] = sum_up(recv_e)
+    start_all(13, send_f, recv_f, same=True)
 
     def fourth_pass(g, carry):
         first = g * GROUP
@@ -433,57 +465,34 @@
 
     lax.fori_loop(0, blocks // GROUP, fourth_pass, 0)
 
-    wait_on(recv_sem, 9, recv_e)
-
-    def add(p, total):
-        return total + recv_e[p].astype(F32)
-
-    total = lax.fori_loop(0, n, add, jnp.zeros((8, LANES), F32), unroll=8)
-    send_f[...] = (total * (1.0 / tokens)).astype(BF)
-    start_all(10, send_f, recv_f, same=True)
-    wait_on(recv_sem, 10, recv_f)
-    halved = [dst.at[piece] for dst in (recv_b, recv_c, recv_row) for piece in range(2)]
-    for phase, dst in enumerate((recv_a, recv_l, *halved, recv_col, recv_e, recv_f)):
+    wait_on(recv_sem, 12, recv_h)
+    send_g[...] = sum_up(recv_h)
+    start_all(14, send_g, recv_g, same=True)
+    wait_on(recv_sem, 13, recv_f)
+    unpack(recv_f, 4, 24)
+    grad_left[...] = collect(0, 24, 2)
+    grad_gating[...] = collect(2, 24, 1)
+    grad_output[...] = collect(3, 24, 1)
+    wait_on(recv_sem, 14, recv_g)
+    unpack(recv_g, 4, 24)
+    grad_right[...] = collect(0, 24, 2)
+    grad_norms[...] = jnp.transpose(collect(2, 24, 1))[:4]
+    halved = [
+        dst.at[piece]
+        for dst in (recv_l, recv_b, recv_c, recv_row, recv_col)
+        for piece in range(2)
+    ]
+    for phase, dst in enumerate((recv_r, *halved, recv_e, recv_h, recv_f, recv_g)):
         wait_on(send_sem, phase, dst)
 
 
-def finish(
-    update_in,
-    grad_pair_in,
-    totals,
-    update,
-    grad_pair,
-    grad_left,
-    grad_right,
-    grad_gating,
-    grad_output,
-    grad_norms,
-    stage,
-    sems,
-):
+def finish(*refs):
+    count = len(refs) // 2
     stores = [
-        pltpu.make_async_copy(update_in, update, sems.at[0]),
-        pltpu.make_async_copy(grad_pair_in, grad_pair, sems.at[1]),
+        pltpu.make_async_copy(refs[t], refs[count + t], refs[-1].at[t]) for t in range(count)
     ]
     for store in stores:
         store.start()
-
-    def unpack(h, carry):
-        at = pl.multiple_of(h * 24, 8)
-        stage[pl.ds(at, 8), :] = totals[h].astype(F32)
-        return carry
-
-    lax.fori_loop(0, LANES, unpack, 0, unroll=8)
-
-    def collect(first):
-        return stage[pl.ds(first, LANES, stride=24), :]
-
-    for t in range(2):
-        grad_left[:, t * LANES : (t + 1) * LANES] = collect(t)
-        grad_right[:, t * LANES : (t + 1) * LANES] = collect(2 + t)
-    grad_gating[...] = collect(4)
-    grad_output[...] = collect(5)
-    grad_norms[...] = jnp.transpose(collect(6))[:4]
     for store in stores:
         store.wait()
 
@@ -500,19 +509,23 @@
     part = blocks // 2
     weights = [w.reshape(1, -1) if w.ndim == 1 else w for w in weights]
     vmem = pl.BlockSpec(memory_space=pltpu.VMEM)
-    smem = pl.BlockSpec(memory_space=pltpu.SMEM)
     shape = jax.ShapeDtypeStruct
     hbm = pl.BlockSpec(memory_space=pl.ANY)
     far = functools.partial(pltpu.with_memory_space_constraint, memory_space=pltpu.HBM)
+    outs = (
+        (pair.shape, BF),
+        (pair.shape, BF),
+        ((chan, 2 * hidden), F32),
+        ((chan, 2 * hidden), F32),
+        ((chan, chan), F32),
+        ((hidden, chan), F32),
+        ((4, chan), F32),
+    )
     raw = pl.pallas_call(
         functools.partial(kernel, n_row, n_col),
-        out_shape=(
-            pltpu.VMEM(pair.shape, BF),
-            pltpu.VMEM(pair.shape, BF),
-            pltpu.VMEM((n, 8, LANES), BF),
-        ),
-        in_specs=[hbm, hbm, smem] + [hbm] * len(weights),
-        out_specs=(vmem,) * 3,
+        out_shape=tuple(pltpu.VMEM(*out) for out in outs),
+        in_specs=[hbm, hbm, pl.BlockSpec(memory_space=pltpu.SMEM)] + [hbm] * len(weights),
+        out_specs=(vmem,) * len(outs),
         scratch_shapes=[
             pltpu.VMEM(pair.shape, BF),
             *[pltpu.VMEM(w.shape, w.dtype) for w in weights[:5]],
@@ -535,14 +548,15 @@
             pltpu.VMEM((2, tokens // 2, tokens), BF),
             pltpu.VMEM((tokens, tokens), BF),
             pltpu.VMEM((tokens, tokens), BF),
-            *[pltpu.VMEM((n, blocks + part, LANES), BF)] * 2,
-            *[pltpu.VMEM((n, part, LANES), BF)] * 2,
-            *[pltpu.VMEM((2, n, part, LANES), BF)] * 6,
             *[pltpu.VMEM((n, blocks, LANES), BF)] * 2,
-            *[pltpu.VMEM((n, 8, LANES), BF)] * 2,
-            pltpu.VMEM((8, LANES), BF),
-            pltpu.SemaphoreType.DMA((11,)),
-            pltpu.SemaphoreType.DMA((11,)),
+            *[pltpu.VMEM((2, n, part, LANES), BF)] * 10,
+            *[pltpu.VMEM((n, 4, LANES), BF)] * 4,
+            pltpu.VMEM((4, LANES), BF),
+            pltpu.VMEM((n, 4, LANES), BF),
+            pltpu.VMEM((4, LANES), BF),
+            pltpu.VMEM((n, 4, LANES), BF),
+            pltpu.SemaphoreType.DMA((15,)),
+            pltpu.SemaphoreType.DMA((15,)),
             pltpu.SemaphoreType.DMA((10,)),
         ],
         compiler_params=pltpu.CompilerParams(
@@ -553,18 +567,10 @@
     raw = [pltpu.with_memory_space_constraint(a, pltpu.VMEM) for a in raw]
     return pl.pallas_call(
         finish,
-        out_shape=(
-            shape(pair.shape, BF),
-            shape(pair.shape, BF),
-            shape((chan, 2 * hidden), F32),
-            shape((chan, 2 * hidden), F32),
-            shape((chan, chan), F32),
-            shape((hidden, chan), F32),
-            shape((4, chan), F32),
-        ),
-        in_specs=[vmem] * 3,
-        out_specs=(hbm, hbm) + (vmem,) * 5,
-        scratch_shapes=[pltpu.VMEM((LANES * 24, LANES), F32), pltpu.SemaphoreType.DMA((2,))],
+        out_shape=tuple(shape(*out) for out in outs),
+        in_specs=[vmem] * len(outs),
+        out_specs=(hbm,) * len(outs),
+        scratch_shapes=[pltpu.SemaphoreType.DMA((len(outs),))],
         compiler_params=pltpu.CompilerParams(vmem_limit_bytes=8 << 20),
         name="finish",
     )(*raw)

time: 75.1 us -> 73.4 us (0.977)
  Pallas kernels: 72.6 us -> 70.9 us
    pallas_call x2, Pallas kernels: 72.6 us -> 70.9 us  [the longest x1 69.7 us: per_device(): pl.pallas_call(functools.partial(kernel, n_row, n_col), out_shape=tuple((...]
where the time goes in v7:
time: 73.4 us; the launch traced here: 72.3 us
  Pallas kernels  70.9 us (97%)
  between operations  1.45 us (2%)
    pallas_call x1, Pallas kernels, per_device(): pl.pallas_call(functools.partial(kernel, n_row, n_col), out_shape=tuple((...  69.7 us

profile of v7, /device:TPU:0, one launch (start us, length us, event | category | flops | bytes accessed | tf_op | source)
XLA Modules:
  0.0 72.3 jit_solution(17742364891832015933)
XLA Ops:
  1.3 69.7 %triangle.1 = (bf16[32,64,128]{2,1,0:T(8,128)(2,1)S(1)}, bf16[32,64,128]{2,1,0:T(8,128)(2,1)S(1)}, f32[128,256]{1,0:T(8,128)S(1)}, f32[128,256]{1,0:T(8,128)S(1)...) custom-call(bf16[32,64,128]{2,1,0:T(8,128)(2,1)} %pair_hbm.1, ...), custom_call_target="tpu_custom_call" | custom-call | tf_op jit(solution)/shard_map/triangle/pallas_call | solution.py:524
  71.0 1.1 %finish.1 = (bf16[32,64,128]{2,1,0:T(8,128)(2,1)}, bf16[32,64,128]{2,1,0:T(8,128)(2,1)}, f32[128,256]{1,0:T(8,128)}, f32[128,256]{1,0:T(8,128)}, f32[128,128]{1,...) custom-call(bf16[32,64,128]{2,1,0:T(8,128)(2,1)S(1)} %get-tuple-element.14.refs_0_, ...), custom_call_target="tpu_custom_call" | custom-call | tf_op jit(solution)/shard_map/finish/pallas_call | solution.py:568

commit v8 on v7

--- a/solution.py
+++ b/solution.py
@@ -212,7 +212,7 @@
             dst[h] = stage[pl.ds(at, count), :].astype(BF)
             return carry
 
-        lax.fori_loop(0, n, body, 0, unroll=8)
+        lax.fori_loop(0, n, body, 0, unroll=16)
 
     def unpack(src, count, stride, first=0):
         def body(h, carry):
@@ -220,7 +220,7 @@
             stage[pl.ds(at, count), :] = src[h].astype(F32)
             return carry
 
-        lax.fori_loop(0, n, body, 0, unroll=8)
+        lax.fori_loop(0, n, body, 0, unroll=16)
 
     def spread(values, first, stride):
         for t in range(values.shape[1] // LANES):
@@ -257,7 +257,7 @@
                 dst[pl.ds(base, 2 * count), q * LANES : (q + 1) * LANES] = both
             return carry
 
-        lax.fori_loop(0, n_row, body, 0, unroll=2)
+        lax.fori_loop(0, n_row, body, 0, unroll=4)
 
     def disassemble(values, count, dst):
         for r in range(n_row):
@@ -435,7 +435,7 @@
             return total + recv[p].astype(F32)
 
         zeros = jnp.zeros(recv.shape[1:], F32)
-        return (lax.fori_loop(0, n, add, zeros, unroll=8) * (1.0 / tokens)).astype(BF)
+        return (lax.fori_loop(0, n, add, zeros, unroll=32) * (1.0 / tokens)).astype(BF)
 
     left_0, _ = through(0, 0, 7, recv_row, left_weight)
     left_1, _ = through(0, 1, 7, recv_row, left_weight)
@@ -531,7 +531,7 @@
             *[pltpu.VMEM(w.shape, w.dtype) for w in weights[:5]],
             pltpu.VMEM(pair.shape, BF),
             *[pltpu.VMEM(w.shape, w.dtype) for w in weights[5:]],
-            pltpu.VMEM((n * 40, LANES), F32),
+            pltpu.VMEM((n * 40 + 64, LANES), F32),
             pltpu.VMEM((chan, places), F32),
             pltpu.VMEM((1, places), F32),
             pltpu.VMEM((chan, places), BF),

time: 73.4 us -> 72.5 us (0.988)
  Pallas kernels: 70.9 us -> 69.9 us
    pallas_call x1, Pallas kernels: 69.7 us -> 68.8 us  [per_device(): pl.pallas_call(functools.partial(kernel, n_row, n_col), out_shape=tuple((...]
where the time goes in v8:
time: 72.5 us; the launch traced here: 71.4 us
  Pallas kernels  69.9 us (96%)
  between operations  1.45 us (2%)
    pallas_call x1, Pallas kernels, per_device(): pl.pallas_call(functools.partial(kernel, n_row, n_col), out_shape=tuple((...  68.8 us

profile of v8, /device:TPU:0, one launch (start us, length us, event | category | flops | bytes accessed | tf_op | source)
XLA Modules:
  0.0 71.4 jit_solution(15788963705551373448)
XLA Ops:
  1.3 68.8 %triangle.1 = (bf16[32,64,128]{2,1,0:T(8,128)(2,1)S(1)}, bf16[32,64,128]{2,1,0:T(8,128)(2,1)S(1)}, f32[128,256]{1,0:T(8,128)S(1)}, f32[128,256]{1,0:T(8,128)S(1)...) custom-call(bf16[32,64,128]{2,1,0:T(8,128)(2,1)} %pair_hbm.1, ...), custom_call_target="tpu_custom_call" | custom-call | tf_op jit(solution)/shard_map/triangle/pallas_call | solution.py:524
  70.1 1.1 %finish.1 = (bf16[32,64,128]{2,1,0:T(8,128)(2,1)}, bf16[32,64,128]{2,1,0:T(8,128)(2,1)}, f32[128,256]{1,0:T(8,128)}, f32[128,256]{1,0:T(8,128)}, f32[128,128]{1,...) custom-call(bf16[32,64,128]{2,1,0:T(8,128)(2,1)S(1)} %get-tuple-element.14.refs_0_, ...), custom_call_target="tpu_custom_call" | custom-call | tf_op jit(solution)/shard_map/finish/pallas_call | solution.py:568
